TPU v7x, 32 devices: a whole 2x2x4 slice. The times are simulated.
32 devices in a mesh: fsdp: 16 (over z, y, x), tp: 2 (over core).
Axes of the slice: x: 2, y: 2, z: 4, core: 2. Of those that a mesh axis runs over, the one named last changes fastest.
Arguments:
- hidden_in: bfloat16 [16384, 1152], P(('fsdp', 'tp')), may hold values from -6 to 6
- out_grad: bfloat16 [16384, 1152], P(('fsdp', 'tp')), may hold values from -6 to 6
- segments: int32 [16384], P('fsdp'), may hold values from 0 to 17, as said below
- positions: int32 [16384], P('fsdp'), may hold values from 0 to 799, as said below
- set_ids: int32 [16], replicated, may hold values from 0 to 7, as said below
- query_w: bfloat16 [2, 1152, 1024], P(None, 'fsdp', 'tp'), may hold values from -0.1875 to 0.1875
- key_w: bfloat16 [2, 1152, 256], P(None, 'fsdp'), may hold values from -0.1875 to 0.1875
- value_w: bfloat16 [2, 1152, 256], P(None, 'fsdp'), may hold values from -0.1875 to 0.1875
- out_w: bfloat16 [2, 1024, 1152], P(None, 'tp', 'fsdp'), may hold values from -0.1875 to 0.1875
- gate_w: bfloat16 [2, 1152, 6912], P(None, 'fsdp', 'tp'), may hold values from -0.1875 to 0.1875
- up_w: bfloat16 [2, 1152, 6912], P(None, 'fsdp', 'tp'), may hold values from -0.1875 to 0.1875
- down_w: bfloat16 [2, 6912, 1152], P(None, 'tp', 'fsdp'), may hold values from -0.078125 to 0.078125
- norm_gains: bfloat16 [2, 4, 1152], replicated, may hold values from -0.3984375 to 0.3984375
- head_gains: bfloat16 [2, 2, 256], replicated, may hold values from -0.3984375 to 0.3984375
- adapters: float32 [8, 1003520], P(None, ('fsdp', 'tp')), may hold values from -0.18 to 0.18
- first_moment: float32 [8, 1003520], P(None, ('fsdp', 'tp')), may hold values from -1122 to 1122
- second_moment: float32 [8, 1003520], P(None, ('fsdp', 'tp')), may hold values from 4371 to 69938
Outputs:
- second_layer_output: bfloat16 [16384, 1152], P(('fsdp', 'tp'))
- input_grad: float32 [16384, 1152], P(('fsdp', 'tp'))
- adapter_grads: float32 [8, 1003520], P(None, ('fsdp', 'tp'))
- new_adapters: float32 [8, 1003520], P(None, ('fsdp', 'tp'))
- new_first: float32 [8, 1003520], P(None, ('fsdp', 'tp'))
- new_second: float32 [8, 1003520], P(None, ('fsdp', 'tp'))
- adapter_copy: bfloat16 [8, 1003520], P(None, ('fsdp', 'tp'))
Inputs may be any that keep to these rules, and one draw needn't show every extreme that they name: `segments`: within each sequence of 1024 tokens the document number starts at 0 and rises by one at each new document; every document that ends inside its sequence has 60 to 800 tokens, the last one of a sequence 1 to 800; some document has exactly 800 tokens, and some sequence holds the most documents that these bounds allow. `positions`: each token's offset from the first token of its document. `set_ids`: every one of the 8 sets is used by at least one sequence.
All inputs are finite; a program needn't handle non-finite values.
Results may differ from a plain program's by a relative error of at most 0.028.
Values may be sent and summed in bfloat16 or wider, within the bound.
A program may use at most 448 MiB of HBM per device.

v0:
```python
import functools
import math

import jax
import jax.numpy as jnp
from jax import lax
from jax.experimental import pallas as pl
from jax.experimental.pallas import tpu as pltpu
from jax.sharding import PartitionSpec as P

D = 1152
HEADS = 4
HD = 256
FF = 6912
WINDOW = 512
RANK = 16
LAYERS = 2
LANES = 128
GROUPS = LANES // RANK

NORM_EPS = 1e-06
ADAPTER_SCALING = 4.0
ROPE_BASE = 10000.0
LEARN_RATE = 0.01
BETA_ONE = 0.5
BETA_TWO = 0.6
ADAM_STEPS = 4.0
ADAM_EPS = 1e-08
DECAY_RATE = 0.1
NEG_FILL = -1e30
F32 = jnp.float32
BF16 = jnp.bfloat16
MESH = pl.DeviceIdType.MESH

PIECES = (
    ("Eq", D), ("Xq", HEADS * HD), ("Ek", D), ("Xk", HD), ("Ev", D), ("Xv", HD),
    ("Eo", HEADS * HD), ("Xo", D), ("Eg", D), ("Xg", FF), ("Eu", D), ("Xu", FF),
    ("Ed", FF), ("Xd", D),
)


def dot(a, b, out=F32):
    return lax.dot_general(a, b, (((1,), (0,)), ((), ())), preferred_element_type=F32).astype(out)


def dot_nt(a, b, out=F32):
    return lax.dot_general(a, b, (((1,), (1,)), ((), ())), preferred_element_type=F32).astype(out)


def dot_tn(a, b, out=F32):
    return lax.dot_general(a, b, (((0,), (0,)), ((), ())), preferred_element_type=F32).astype(out)


def rms(v, gain):
    return v * lax.rsqrt(jnp.mean(v * v, axis=-1, keepdims=True) + NORM_EPS) * (1.0 + gain)


def rms_back(v, gain, dy):
    r = lax.rsqrt(jnp.mean(v * v, axis=-1, keepdims=True) + NORM_EPS)
    scaled = (1.0 + gain) * dy
    return r * scaled - v * (r * r * r) * jnp.mean(v * scaled, axis=-1, keepdims=True)


def exchange_kernel(body, has_partial, n_rows, n_gains, n_outs, has_send, n_chunks, *refs):
    refs = list(refs)
    partial = refs.pop(0) if has_partial else None
    rows = [refs.pop(0) for _ in range(n_rows)]
    gains = [refs.pop(0) for _ in range(n_gains)]
    outs = [refs.pop(0) for _ in range(n_outs)]
    gathered = refs.pop(0) if has_send else None
    if has_partial:
        arrived, send_a, recv_a = refs[:3]
        refs = refs[3:]
    if has_send:
        send_b, recv_b = refs[:2]
    me = lax.axis_index("tp")
    other = 1 - me
    barrier = pltpu.get_barrier_semaphore()
    pl.semaphore_signal(barrier, inc=1, device_id={"tp": other}, device_id_type=MESH)
    pl.semaphore_wait(barrier, 1)
    half = (partial if has_partial else gathered).shape[0] // 2
    chunk = half // n_chunks

    def span(base, c):
        return pl.ds(pl.multiple_of(base * half + c * chunk, chunk), chunk)

    sends = []
    if has_partial:
        for c in range(n_chunks):
            copy = pltpu.make_async_remote_copy(
                src_ref=partial.at[span(other, c)],
                dst_ref=arrived.at[pl.ds(c * chunk, chunk)],
                send_sem=send_a.at[c],
                recv_sem=recv_a.at[c],
                device_id={"tp": other},
                device_id_type=MESH,
            )
            copy.start()
            sends.append(copy)
    gain_values = [g[...].astype(F32) for g in gains]
    spreads = []
    for c in range(n_chunks):
        local = pl.ds(c * chunk, chunk)
        total = None
        if has_partial:
            sends[c].wait_recv()
            total = partial[span(me, c), :].astype(F32) + arrived[local, :].astype(F32)
        values, spread = body(total, [r[local, :].astype(F32) for r in rows], gain_values)
        for ref, value in zip(outs, values):
            ref[local, :] = value.astype(ref.dtype)
        if has_send:
            gathered[span(me, c), :] = spread.astype(BF16)
            spreads.append(
                pltpu.make_async_remote_copy(
                    src_ref=gathered.at[span(me, c)],
                    dst_ref=gathered.at[span(me, c)],
                    send_sem=send_b.at[c],
                    recv_sem=recv_b.at[c],
                    device_id={"tp": other},
                    device_id_type=MESH,
                )
            )
            if c > 0:
                spreads[c - 1].start()
    if has_send:
        spreads[-1].start()
    for copy in sends:
        copy.wait_send()
    for copy in spreads:
        copy.wait()


def exchange(body, collective_id, name, partial, rows, gains, out_types, has_send, n_chunks=4):
    operands = ([] if partial is None else [partial]) + list(rows) + list(gains)
    width = operands[0].shape[1]
    half = partial.shape[0] // 2 if partial is not None else rows[0].shape[0]
    outs = [jax.ShapeDtypeStruct((half, width), kind) for kind in out_types]
    if has_send:
        outs.append(jax.ShapeDtypeStruct((2 * half, width), BF16))
    scratch = []
    if partial is not None:
        scratch += [
            pltpu.VMEM((half, width), partial.dtype),
            pltpu.SemaphoreType.DMA((n_chunks,)),
            pltpu.SemaphoreType.DMA((n_chunks,)),
        ]
    if has_send:
        scratch += [pltpu.SemaphoreType.DMA((n_chunks,)), pltpu.SemaphoreType.DMA((n_chunks,))]
    vmem = pl.BlockSpec(memory_space=pltpu.VMEM)
    return pl.pallas_call(
        functools.partial(
            exchange_kernel, body, partial is not None, len(rows), len(gains), len(out_types),
            has_send, n_chunks,
        ),
        out_shape=outs,
        in_specs=[vmem] * len(operands),
        out_specs=[vmem] * len(outs),
        scratch_shapes=scratch,
        compiler_params=pltpu.CompilerParams(collective_id=collective_id, has_side_effects=True),
        name=name,
    )(*operands)


def gather_kernel(plan, nz, rows, n_arrays, *refs):
    mine, gathered = refs[:n_arrays], refs[n_arrays : 2 * n_arrays]
    send_sem, recv_sem, local_sem = refs[2 * n_arrays :]
    f = lax.axis_index("fsdp")
    x, y, z = f % 2, (f // 2) % 2, f // 4

    def index(a, b, c):
        return (a * 2 + b) * 2 + c

    peers = {
        "x": (index(z, y, 1 - x), None),
        "y": (index(z, 1 - y, x), None),
        "u": (f + 4, z < nz - 1),
        "d": (f - 4, z > 0),
    }
    ways_index = "xyud".index

    def guarded(cond, fn):
        if cond is None:
            fn()
        else:
            pl.when(cond)(fn)

    barrier = pltpu.get_barrier_semaphore()

    def greet(peer):
        pl.semaphore_signal(barrier, inc=1, device_id={"fsdp": peer}, device_id_type=MESH)

    for peer, cond in peers.values():
        guarded(cond, functools.partial(greet, peer))
    inside = jnp.logical_and(z > 0, z < nz - 1)
    pl.when(inside)(lambda: pl.semaphore_wait(barrier, 4))
    pl.when(jnp.logical_not(inside))(lambda: pl.semaphore_wait(barrier, 3))

    offsets = [(dz, fy, fx) for dz in range(1 - nz, nz) for fy in (0, 1) for fx in (0, 1)]
    offsets.sort(key=lambda o: (abs(o[0]) + o[1] + o[2], o))
    ids = {o: i for i, o in enumerate(offsets)}
    own = (0, 0, 0)

    def place(array, source, columns):
        return gathered[array].at[pl.ds(pl.multiple_of(source * rows, 8), rows), pl.ds(*columns)]

    for a in range(n_arrays):
        pltpu.make_async_copy(
            mine[a], place(a, f, (0, mine[a].shape[1])), local_sem.at[a]
        ).start()

    def source_of(o):
        return index(z + o[0], y + o[1] - 2 * y * o[1], x + o[2] - 2 * x * o[2])

    def copy(k, o, way):
        target = {
            "u": (o[0] - 1, o[1], o[2]), "d": (o[0] + 1, o[1], o[2]),
            "x": (o[0], o[1], 1), "y": (o[0], 1, o[2]),
        }[way]
        _, array, columns = plan[k]
        block = place(array, source_of(o), columns)
        return pltpu.make_async_remote_copy(
            src_ref=mine[array].at[:, pl.ds(*columns)] if o == own else block,
            dst_ref=block,
            send_sem=send_sem.at[k, ids[o], ways_index(way)],
            recv_sem=recv_sem.at[k, ids[target]],
            device_id={"fsdp": peers[way][0]},
            device_id_type=MESH,
        )

    def arrival(k, o):
        _, array, columns = plan[k]
        block = place(array, source_of(o), columns)
        return pltpu.make_async_remote_copy(
            src_ref=block, dst_ref=block, send_sem=send_sem.at[k, ids[o], 0],
            recv_sem=recv_sem.at[k, ids[o]], device_id={"fsdp": peers["x"][0]}, device_id_type=MESH,
        )

    def ways(order, o):
        used = {"z": o[0] != 0, "y": o[1] != 0, "x": o[2] != 0}
        last = max([i for i, a in enumerate(order) if used[a]], default=-1)
        out = []
        if last >= 0 and order[last] == "z" and abs(o[0]) < nz - 1:
            out.append("d" if o[0] > 0 else "u")
        for a in order[last + 1 :]:
            out += ["u", "d"] if a == "z" else [a]
        return out

    def exists(o):
        if o[0] == 0:
            return None
        return z < nz - o[0] if o[0] > 0 else z >= -o[0]

    def pass_on(k, o):
        if o != own:
            arrival(k, o).wait_recv()
        for way in ways(plan[k][0], o):
            guarded(peers[way][1], lambda way=way: copy(k, o, way).start())

    def finish(k, o):
        for way in ways(plan[k][0], o):
            guarded(peers[way][1], lambda way=way: copy(k, o, way).wait_send())

    for step in (pass_on, finish):
        for o in offsets:
            for k in range(len(plan)):
                guarded(exists(o), functools.partial(step, k, o))
    for a in range(n_arrays):
        pltpu.make_async_copy(
            mine[a], place(a, f, (0, mine[a].shape[1])), local_sem.at[a]
        ).wait()


def gather_weights(arrays, plan, count, collective_id):
    rows = arrays[0].shape[0]
    nz = count // 4
    offsets = (2 * nz - 1) * 4
    return pl.pallas_call(
        functools.partial(gather_kernel, plan, nz, rows, len(arrays)),
        out_shape=[
            jax.ShapeDtypeStruct((count * rows, a.shape[1]), a.dtype) for a in arrays
        ],
        in_specs=[pl.BlockSpec(memory_space=pltpu.VMEM)] * len(arrays),
        out_specs=[pl.BlockSpec(memory_space=pl.ANY)] * len(arrays),
        scratch_shapes=[
            pltpu.SemaphoreType.DMA((len(plan), offsets, 4)),
            pltpu.SemaphoreType.DMA((len(plan), offsets)),
            pltpu.SemaphoreType.DMA((len(arrays),)),
        ],
        compiler_params=pltpu.CompilerParams(collective_id=collective_id, has_side_effects=True),
        name="gather_weights",
    )(*arrays)


def pair_sum_kernel(count, partial, total, arrived, send_sem, recv_sem):
    me = lax.axis_index("tp")
    other = 1 - me
    barrier = pltpu.get_barrier_semaphore()
    pl.semaphore_signal(barrier, inc=1, device_id={"tp": other}, device_id_type=MESH)
    pl.semaphore_wait(barrier, 1)
    copies = []
    for i in range(count):
        copy = pltpu.make_async_remote_copy(
            src_ref=partial.at[2 * i + other], dst_ref=arrived.at[i], send_sem=send_sem.at[i],
            recv_sem=recv_sem.at[i], device_id={"tp": other}, device_id_type=MESH,
        )
        copy.start()
        copies.append(copy)
    for i in range(count):
        copies[i].wait_recv()
        total[i] = (partial[2 * i + me].astype(F32) + arrived[i].astype(F32)).astype(total.dtype)
    for copy in copies:
        copy.wait_send()


def pair_sum(partial, collective_id):
    count = partial.shape[0] // 2
    shape = (count,) + partial.shape[1:]
    vmem = pl.BlockSpec(memory_space=pltpu.VMEM)
    return pl.pallas_call(
        functools.partial(pair_sum_kernel, count),
        out_shape=jax.ShapeDtypeStruct(shape, partial.dtype),
        in_specs=[vmem],
        out_specs=vmem,
        scratch_shapes=[
            pltpu.VMEM(shape, partial.dtype),
            pltpu.SemaphoreType.DMA((count,)),
            pltpu.SemaphoreType.DMA((count,)),
        ],
        compiler_params=pltpu.CompilerParams(collective_id=collective_id, has_side_effects=True),
        name="pair_sum",
    )(partial)


def body_enter(total, rows, gains):
    return [], rms(rows[0], gains[0])


def body_middle(total, rows, gains):
    middle = rows[0] + rms(total, gains[0])
    return [total, middle], rms(middle, gains[1])


def body_next(total, rows, gains):
    leaving = rows[0] + rms(total, gains[0])
    return [total, leaving], rms(leaving, gains[1])


def body_turn(total, rows, gains):
    leaving = rows[0] + rms(total, gains[0])
    return [leaving], rms_back(total, gains[0], rows[1])


def body_back_middle(total, rows, gains):
    grad_middle = rows[0] + rms_back(rows[1], gains[0], total)
    return [grad_middle], rms_back(rows[2], gains[1], grad_middle)


def body_back_next(total, rows, gains):
    grad_x = rows[0] + rms_back(rows[1], gains[0], total)
    return [grad_x], rms_back(rows[2], gains[1], grad_x)


def body_back_last(total, rows, gains):
    return [rows[0] + rms_back(rows[1], gains[0], total)], None


def lane_group_mask(count):
    row = lax.broadcasted_iota(jnp.int32, (count, LANES), 0)
    lane = lax.broadcasted_iota(jnp.int32, (count, LANES), 1)
    return (lane // RANK) == (row % GROUPS)


def expand_entry(flat_rows):
    count = flat_rows.shape[0] * GROUPS
    spread = jnp.broadcast_to(flat_rows[:, None, :], (flat_rows.shape[0], GROUPS, LANES))
    return jnp.where(lane_group_mask(count), spread.reshape(count, LANES), 0).astype(BF16)


def slot_pick(slot):
    row = lax.broadcasted_iota(jnp.int32, (LANES, LANES), 0)
    lane = lax.broadcasted_iota(jnp.int32, (LANES, LANES), 1)
    return (lane == slot * RANK + row % RANK).astype(BF16)


def slot_spread(slot):
    row = lax.broadcasted_iota(jnp.int32, (LANES, LANES), 0)
    lane = lax.broadcasted_iota(jnp.int32, (LANES, LANES), 1)
    return (row == slot * RANK + lane % RANK).astype(BF16)


def in_slot(rows, slot):
    return jnp.pad(rows, ((slot * RANK, LANES - (slot + 1) * RANK), (0, 0)))


def rope_tables(positions):
    half = HD // 2
    frequency = jnp.exp(jnp.arange(half, dtype=F32) * (-2.0 * math.log(ROPE_BASE) / HD))
    angles = positions.astype(F32)[:, None] * frequency[None, :]
    return jnp.cos(angles), jnp.sin(angles)


def head_forward(raw, gain, cosine, sine):
    n = rms(raw, gain)
    half = HD // 2
    a, b = n[:, :half], n[:, half:]
    return jnp.concatenate([a * cosine - b * sine, b * cosine + a * sine], axis=1)


def head_backward(raw, gain, cosine, sine, grad):
    half = HD // 2
    a, b = grad[:, :half], grad[:, half:]
    turned = jnp.concatenate([a * cosine + b * sine, b * cosine - a * sine], axis=1)
    return rms_back(raw, gain, turned)


ROW_BLOCK = 256
VMEM_LIMIT = 67000000
KEY_SPAN = WINDOW + ROW_BLOCK


def rows_at(i, count=ROW_BLOCK):
    return pl.ds(pl.multiple_of(i * count, count), count)


def key_start(i):
    return pl.multiple_of(jnp.maximum(i * ROW_BLOCK - WINDOW, 0), ROW_BLOCK)


def allowed_keys(i, first, segment_column, segment_row):
    rows = i * ROW_BLOCK + lax.broadcasted_iota(jnp.int32, (ROW_BLOCK, KEY_SPAN), 0)
    keys = first + lax.broadcasted_iota(jnp.int32, (ROW_BLOCK, KEY_SPAN), 1)
    gap = rows - keys
    same = segment_column[rows_at(i), :] == segment_row[:, pl.ds(first, KEY_SPAN)]
    return (gap >= 0) & (gap < WINDOW) & same


def weight_copies(sources, target, sems, columns=None):
    out, at = [], 0
    for i, source in enumerate(sources):
        count = source.shape[0]
        part = source if columns is None else source.at[:, columns]
        out.append(pltpu.make_async_copy(part, target.at[pl.ds(at, count)], sems.at[i]))
        at += count
    return out


def with_slots(weight):
    return pltpu.VMEM((weight.shape[0] + LANES, weight.shape[1]), BF16)


def attention_forward_kernel(
    local_heads, scale, normed, enter, leave, gains, cosine, sine, segment_column, segment_row,
    w_qkv, w_o, s_qkv, s_o, raw, qkv, attn, mid_qkv, mid_o, stats, share, w_qkv_here, w_o_here, sems,
):
    copies = [
        weight_copies((w_qkv, s_qkv), w_qkv_here, sems.at[0]),
        weight_copies((w_o, s_o), w_o_here, sems.at[1]),
    ]
    for c in copies[0] + copies[1]:
        c.start()
    blocks = normed.shape[0] // ROW_BLOCK
    key_col = local_heads * HD
    value_col = key_col + HD
    for c in copies[0]:
        c.wait()

    @pl.loop(0, blocks)
    def _(i):
        rows = rows_at(i)
        z = normed[rows, :]
        mid = dot(z, enter[...], BF16)
        mid_qkv[rows, :] = mid
        full = dot(jnp.concatenate([z, mid], axis=1), w_qkv_here[...])
        c, s = cosine[rows, :], sine[rows, :]
        for h in range(local_heads + 1):
            columns = slice(h * HD, (h + 1) * HD)
            gain = gains[0:1, :] if h < local_heads else gains[1:2, :]
            qkv[rows, columns] = head_forward(full[:, columns], gain, c, s).astype(BF16)
        raw[rows, :] = full[:, :value_col]
        qkv[rows, value_col:] = full[:, value_col:].astype(BF16)

    for c in copies[1]:
        c.wait()

    @pl.loop(0, blocks)
    def _(i):
        rows = rows_at(i)
        first = key_start(i)
        keys = qkv[pl.ds(first, KEY_SPAN), key_col:value_col]
        values = qkv[pl.ds(first, KEY_SPAN), value_col:]
        mask = allowed_keys(i, first, segment_column, segment_row)
        for h in range(local_heads):
            scores = dot_nt(qkv[rows, h * HD : (h + 1) * HD], keys) * scale
            scores = jnp.where(mask, scores, NEG_FILL)
            top = jnp.max(scores, axis=-1, keepdims=True)
            expon = jnp.exp(scores - top)
            total = jnp.sum(expon, axis=-1, keepdims=True)
            probs = (expon / total).astype(BF16)
            attn[rows, h * HD : (h + 1) * HD] = dot(probs, values, BF16)
            stats[rows, h * LANES : (h + 1) * LANES] = jnp.broadcast_to(
                top + jnp.log(total), (ROW_BLOCK, LANES)
            )
        both = dot_nt(attn[rows, :], w_o_here[...])
        mid = both[:, -LANES:].astype(BF16)
        mid_o[rows, :] = mid
        share[rows, :] = (both[:, :-LANES] + dot(mid, leave[...])).astype(BF16)


def attention_forward(normed, enter, leave, gains, cosine, sine, segments, qkv_parts, o_parts, scale):
    w_qkv, w_o = qkv_parts[0], o_parts[0]
    length, width = normed.shape
    columns = w_qkv.shape[1]
    local_heads = columns // HD - 2
    shapes = [
        ((length, columns - HD), F32), ((length, columns), BF16), ((length, local_heads * HD), BF16),
        ((length, LANES), BF16), ((length, LANES), BF16), ((length, local_heads * LANES), F32),
        ((length, width), BF16),
    ]
    vmem = pl.BlockSpec(memory_space=pltpu.VMEM)
    return pl.pallas_call(
        functools.partial(attention_forward_kernel, local_heads, scale),
        out_shape=[jax.ShapeDtypeStruct(*shape) for shape in shapes],
        in_specs=[vmem] * 8 + [pl.BlockSpec(memory_space=pl.ANY)] * 4,
        out_specs=[vmem] * len(shapes),
        scratch_shapes=[
            with_slots(w_qkv), with_slots(w_o), pltpu.SemaphoreType.DMA((2, 2)),
        ],
        name="attention_forward",
    )(normed, enter, leave, gains, cosine, sine, segments[:, None], segments[None, :], w_qkv, w_o,
        qkv_parts[1], o_parts[1])


def fold_rows(wide):
    row = lax.broadcasted_iota(jnp.int32, wide.shape, 0)
    lane = lax.broadcasted_iota(jnp.int32, wide.shape, 1)
    kept = jnp.where((lane % LANES) // RANK == row % GROUPS, wide, 0.0)
    return jnp.sum(kept.reshape(wide.shape[0] // GROUPS, GROUPS, wide.shape[1]), axis=1).astype(BF16)


def attention_backward_kernel(
    local_heads, scale, grad_branch, enter, leave, gains, cosine, sine, segment_column, segment_row,
    spread, raw, qkv, attn, stats, normed, mid_qkv, mid_o, w_qkv, w_o, s_qkv, s_o,
    share, entry_qkv, entry_o, exit_qkv, exit_o,
    w_qkv_here, w_o_here, grad_attn, grad_raw, grad_k, grad_v, spread_qkv, spread_o, sems,
):
    copies = [
        weight_copies((w_o, s_o), w_o_here, sems.at[0]),
        weight_copies((w_qkv, s_qkv), w_qkv_here, sems.at[1]),
    ]
    for c in copies[0] + copies[1]:
        c.start()
    blocks = normed.shape[0] // ROW_BLOCK
    key_col = local_heads * HD
    value_col = key_col + HD
    grad_k[...] = jnp.zeros_like(grad_k)
    grad_v[...] = jnp.zeros_like(grad_v)
    for c in copies[0]:
        c.wait()

    @pl.loop(0, blocks)
    def _(i):
        rows = rows_at(i)
        g = grad_branch[rows, :]
        mid = dot_nt(g, leave[...], BF16)
        spread_o[rows, :] = dot(mid, spread[:, :LANES], BF16)
        grad_attn[rows, :] = dot(jnp.concatenate([g, mid], axis=1), w_o_here[...], BF16)

    @pl.loop(0, blocks)
    def _(i):
        rows = rows_at(i)
        first = key_start(i)
        span = pl.ds(first, KEY_SPAN)
        keys = qkv[span, key_col:value_col]
        values = qkv[span, value_col:]
        mask = allowed_keys(i, first, segment_column, segment_row)
        for h in range(local_heads):
            columns = slice(h * HD, (h + 1) * HD)
            q = qkv[rows, columns]
            g = grad_attn[rows, columns]
            scores = jnp.where(mask, dot_nt(q, keys) * scale, NEG_FILL)
            probs = jnp.exp(scores - stats[rows, h * LANES : h * LANES + 1])
            grad_probs = dot_nt(g, values)
            inner = jnp.sum(probs * grad_probs, axis=-1, keepdims=True)
            grad_scores = (probs * (grad_probs - inner)).astype(BF16)
            grad_q = dot(grad_scores, keys) * scale
            grad_k[span, :] += dot_tn(grad_scores, q) * scale
            grad_v[span, :] += dot_tn(probs.astype(BF16), g)
            grad_raw[rows, columns] = head_backward(
                raw[rows, columns], gains[0:1, :], cosine[rows, :], sine[rows, :], grad_q
            ).astype(BF16)

    for c in copies[1]:
        c.wait()

    @pl.loop(0, blocks)
    def _(i):
        rows = rows_at(i)
        grad_raw[rows, key_col:value_col] = head_backward(
            raw[rows, key_col:value_col], gains[1:2, :], cosine[rows, :], sine[rows, :], grad_k[rows, :]
        ).astype(BF16)
        grad_raw[rows, value_col:] = grad_v[rows, :].astype(BF16)
        both = dot_nt(grad_raw[rows, :], w_qkv_here[...])
        mid = both[:, -LANES:].astype(BF16)
        spread_qkv[rows, :] = dot(mid, spread[...], BF16)
        share[rows, :] = (both[:, :-LANES] + dot_nt(mid, enter[...])).astype(BF16)

    @pl.loop(0, normed.shape[1] // LANES)
    def _(j):
        wide = dot_tn(normed[:, rows_at(j, LANES)], spread_qkv[...])
        entry_qkv[rows_at(j, RANK), :] = fold_rows(wide)

    @pl.loop(0, attn.shape[1] // LANES)
    def _(j):
        wide = dot_tn(attn[:, rows_at(j, LANES)], spread_o[...])
        entry_o[rows_at(j, RANK), :] = fold_rows(wide)

    exits = (ADAPTER_SCALING * dot_tn(mid_qkv[...], grad_raw[...])).astype(BF16)
    exit_qkv[:, :key_col] = exits[:RANK, :key_col]
    exit_qkv[:, key_col:value_col] = exits[RANK : 2 * RANK, key_col:value_col]
    exit_qkv[:, value_col:] = exits[2 * RANK : 3 * RANK, value_col:]
    exit_o[...] = (ADAPTER_SCALING * dot_tn(mid_o[...], grad_branch[...]))[:RANK].astype(BF16)


def attention_backward(
    grad_branch, enter, leave, gains, cosine, sine, segments, kept, qkv_parts, o_parts, scale
):
    w_qkv, w_o = qkv_parts[0], o_parts[0]
    length, width = grad_branch.shape
    columns = w_qkv.shape[1]
    local_heads = columns // HD - 2
    spread = jnp.concatenate([slot_spread(i) for i in range(3)], axis=1)
    shapes = [
        (length, width), (width // GROUPS, 3 * LANES), (local_heads * HD // GROUPS, LANES),
        (RANK, columns), (RANK, width),
    ]
    vmem = pl.BlockSpec(memory_space=pltpu.VMEM)
    return pl.pallas_call(
        functools.partial(attention_backward_kernel, local_heads, scale),
        out_shape=[jax.ShapeDtypeStruct(shape, BF16) for shape in shapes],
        in_specs=[vmem] * 16 + [pl.BlockSpec(memory_space=pl.ANY)] * 4,
        out_specs=[vmem] * len(shapes),
        scratch_shapes=[
            with_slots(w_qkv), with_slots(w_o),
            pltpu.VMEM((length, local_heads * HD), BF16), pltpu.VMEM((length, columns), BF16),
            pltpu.VMEM((length, HD), F32), pltpu.VMEM((length, HD), F32),
            pltpu.VMEM((length, 3 * LANES), BF16), pltpu.VMEM((length, LANES), BF16),
            pltpu.SemaphoreType.DMA((2, 2)),
        ],
        name="attention_backward",
    )(
        grad_branch, enter, leave, gains, cosine, sine, segments[:, None], segments[None, :], spread,
        kept["raw"], kept["qkv"], kept["attn"], kept["stats"], kept["normed"], kept["mid_qkv"],
        kept["mid_o"], w_qkv, w_o, qkv_parts[1], o_parts[1],
    )


def gelu_parts(v):
    c = math.sqrt(2.0 / math.pi)
    th = jnp.tanh(c * (v + 0.044715 * v * v * v))
    value = 0.5 * v * (1.0 + th)
    slope = 0.5 * (1.0 + th) + 0.5 * v * (1.0 - th * th) * (c * (1.0 + 3.0 * 0.044715 * v * v))
    return value, slope


FFN_BLOCK = 1152


def ffn_fetch(weights, offsets, buffers, sems, j, slot):
    out = []
    for k in range(3):
        source, slots = weights[2 * k], weights[2 * k + 1]
        here = buffers.at[k, slot]
        start = pl.multiple_of(j * FFN_BLOCK, LANES)
        rows = source.shape[0]
        out.append(pltpu.make_async_copy(
            source.at[:, pl.ds(offsets[k] + start, FFN_BLOCK)], here.at[pl.ds(0, rows)], sems.at[k, slot, 0]
        ))
        out.append(pltpu.make_async_copy(
            slots.at[:, pl.ds(start, FFN_BLOCK)], here.at[pl.ds(rows, LANES)], sems.at[k, slot, 1]
        ))
    return out


def ffn_step(weights, offsets, buffers, sems, steps):
    j = pl.program_id(0)
    slot = j % 2

    @pl.when(j == 0)
    def _():
        for c in ffn_fetch(weights, offsets, buffers, sems, 0, 0):
            c.start()

    for c in ffn_fetch(weights, offsets, buffers, sems, j, slot):
        c.wait()

    @pl.when(j + 1 < steps)
    def _():
        for c in ffn_fetch(weights, offsets, buffers, sems, j + 1, 1 - slot):
            c.start()

    return slot


def ffn_forward_kernel(
    offsets, steps, z, enter, leave, w_g, s_g, w_u, s_u, w_d, s_d,
    gelu, slope, hidden, mid_gu, mid_d, share, buffers, joined, total, sems,
):
    j = pl.program_id(0)
    width = z.shape[1]
    blocks = z.shape[0] // ROW_BLOCK
    slot = ffn_step((w_g, s_g, w_u, s_u, w_d, s_d), offsets, buffers, sems, steps)

    @pl.when(j == 0)
    def _():
        mid = dot(z[...], enter[...], BF16)
        mid_gu[...] = mid
        joined[:, :width] = z[...]
        joined[:, width:] = mid

    @pl.loop(0, blocks)
    def _(i):
        rows = rows_at(i)
        gate_pre = dot(joined[rows, :], buffers[0, slot])
        up_pre = dot(joined[rows, :], buffers[1, slot])
        value, rate = gelu_parts(gate_pre)
        gelu[rows, :] = value.astype(BF16)
        slope[rows, :] = (rate * up_pre).astype(BF16)
        hidden[rows, :] = (value * up_pre).astype(BF16)

    part = dot_nt(hidden[...], buffers[2, slot])

    @pl.when(j == 0)
    def _():
        total[...] = part

    @pl.when(j > 0)
    def _():
        total[...] += part

    @pl.when(j == steps - 1)
    def _():
        mid = total[:, width:].astype(BF16)
        mid_d[...] = mid
        share[...] = (total[:, :width] + dot(mid, leave[...])).astype(BF16)


def ffn_forward(z, enter, leave, weights, offsets):
    length, width = z.shape
    columns = weights[1].shape[1]
    steps = columns // FFN_BLOCK

    def fixed(shape):
        return pl.BlockSpec(shape, lambda j: (0, 0), pipeline_mode=pl.Buffered(1))

    wide = pl.BlockSpec((length, FFN_BLOCK), lambda j: (0, j))
    hbm = pl.BlockSpec(memory_space=pl.ANY)
    small = (length, LANES)
    return pl.pallas_call(
        functools.partial(ffn_forward_kernel, offsets, steps),
        grid=(steps,),
        out_shape=[jax.ShapeDtypeStruct((length, columns), BF16)] * 3
        + [jax.ShapeDtypeStruct(small, BF16)] * 2
        + [jax.ShapeDtypeStruct((length, width), BF16)],
        in_specs=[fixed(z.shape), fixed(enter.shape), fixed(leave.shape)] + [hbm] * 6,
        out_specs=[wide] * 3 + [fixed(small), fixed(small), fixed((length, width))],
        scratch_shapes=[
            pltpu.VMEM((3, 2, width + LANES, FFN_BLOCK), BF16),
            pltpu.VMEM((length, width + LANES), BF16),
            pltpu.VMEM((length, width + LANES), F32),
            pltpu.SemaphoreType.DMA((3, 2, 2)),
        ],
        compiler_params=pltpu.CompilerParams(vmem_limit_bytes=VMEM_LIMIT),
        name="ffn_forward",
    )(z, enter, leave, *weights)


def ffn_backward_kernel(
    offsets, steps, grad, z, enter, leave, mid_gu, mid_d, spread, gelu, slope, hidden,
    w_g, s_g, w_u, s_u, w_d, s_d,
    share, exit_g, exit_u, entry_d, exit_d, entry_gu,
    buffers, joined, grad_g, grad_u, total, spread_d, spread_gu, sems,
):
    j = pl.program_id(0)
    width = z.shape[1]
    blocks = z.shape[0] // ROW_BLOCK
    slot = ffn_step((w_g, s_g, w_u, s_u, w_d, s_d), offsets, buffers, sems, steps)

    @pl.when(j == 0)
    def _():
        mid = dot_nt(grad[...], leave[...], BF16)
        joined[:, :width] = grad[...]
        joined[:, width:] = mid
        spread_d[...] = dot(mid, spread[:, :LANES], BF16)
        exit_d[...] = (ADAPTER_SCALING * dot_tn(mid_d[...], grad[...]))[:RANK].astype(BF16)

    @pl.loop(0, blocks)
    def _(i):
        rows = rows_at(i)
        grad_hidden = dot(joined[rows, :], buffers[2, slot])
        grad_g[rows, :] = (grad_hidden * slope[rows, :].astype(F32)).astype(BF16)
        grad_u[rows, :] = (grad_hidden * gelu[rows, :].astype(F32)).astype(BF16)

    part = dot_nt(grad_g[...], buffers[0, slot]) + dot_nt(grad_u[...], buffers[1, slot])

    @pl.when(j == 0)
    def _():
        total[...] = part

    @pl.when(j > 0)
    def _():
        total[...] += part

    exit_g[...] = (ADAPTER_SCALING * dot_tn(mid_gu[...], grad_g[...]))[:RANK].astype(BF16)
    exit_u[...] = (ADAPTER_SCALING * dot_tn(mid_gu[...], grad_u[...]))[RANK : 2 * RANK].astype(BF16)

    @pl.loop(0, FFN_BLOCK // LANES)
    def _(i):
        wide = dot_tn(hidden[:, rows_at(i, LANES)], spread_d[...])
        entry_d[rows_at(i, RANK), :] = fold_rows(wide)

    @pl.when(j == steps - 1)
    def _():
        mid = total[:, width:].astype(BF16)
        share[...] = (total[:, :width] + dot_nt(mid, enter[...])).astype(BF16)
        spread_gu[...] = dot(mid, spread[...], BF16)

        @pl.loop(0, width // LANES)
        def _(i):
            wide = dot_tn(z[:, rows_at(i, LANES)], spread_gu[...])
            entry_gu[rows_at(i, RANK), :] = fold_rows(wide)


def ffn_backward(grad, z, enter, leave, kept, weights, offsets):
    length, width = z.shape
    columns = weights[1].shape[1]
    steps = columns // FFN_BLOCK
    spread = jnp.concatenate([slot_spread(i) for i in range(2)], axis=1)

    def fixed(shape):
        return pl.BlockSpec(shape, lambda j: (0, 0), pipeline_mode=pl.Buffered(1))

    wide = pl.BlockSpec((length, FFN_BLOCK), lambda j: (0, j))
    hbm = pl.BlockSpec(memory_space=pl.ANY)
    small = (length, LANES)
    shapes = [
        (length, width), (RANK, columns), (RANK, columns), (columns // GROUPS, LANES), (RANK, width),
        (width // GROUPS, 2 * LANES),
    ]
    narrow = pl.BlockSpec((RANK, FFN_BLOCK), lambda j: (0, j))
    return pl.pallas_call(
        functools.partial(ffn_backward_kernel, offsets, steps),
        grid=(steps,),
        out_shape=[jax.ShapeDtypeStruct(shape, BF16) for shape in shapes],
        in_specs=[
            fixed(grad.shape), fixed(z.shape), fixed(enter.shape), fixed(leave.shape), fixed(small),
            fixed(small), fixed(spread.shape), wide, wide, wide,
        ] + [hbm] * 6,
        out_specs=[
            fixed((length, width)), narrow, narrow,
            pl.BlockSpec((FFN_BLOCK // GROUPS, LANES), lambda j: (j, 0)),
            fixed((RANK, width)), fixed((width // GROUPS, 2 * LANES)),
        ],
        scratch_shapes=[
            pltpu.VMEM((3, 2, width + LANES, FFN_BLOCK), BF16),
            pltpu.VMEM((length, width + LANES), BF16),
            pltpu.VMEM((length, FFN_BLOCK), BF16),
            pltpu.VMEM((length, FFN_BLOCK), BF16),
            pltpu.VMEM((length, width + LANES), F32),
            pltpu.VMEM(small, BF16),
            pltpu.VMEM((length, 2 * LANES), BF16),
            pltpu.SemaphoreType.DMA((3, 2, 2)),
        ],
        compiler_params=pltpu.CompilerParams(vmem_limit_bytes=VMEM_LIMIT),
        name="ffn_backward",
    )(
        grad, z, enter, leave, kept["mid_gu"], kept["mid_d"], spread, kept["gelu"], kept["slope"],
        kept["hidden"], *weights,
    )


def shards(
    hidden_in, out_grad, segments, positions, set_ids, query_w, key_w, value_w, out_w, gate_w,
    up_w, down_w, norm_gains, head_gains, adapters, first_moment, second_moment,
):
    tp_count = lax.axis_size("tp")
    fsdp_count = lax.axis_size("fsdp")
    tp_place = lax.axis_index("tp")
    set_count, share = adapters.shape
    head_cols = HEADS * HD // tp_count
    hidden_cols = FF // tp_count
    scale = HD ** (-0.5)
    set_range = jnp.arange(set_count, dtype=jnp.int32)

    master_low = adapters.astype(BF16)
    owner_sets = jnp.repeat(set_ids, tp_count)
    selector = (owner_sets[:, None] == set_range[None, :]).astype(BF16)
    routed = dot(selector, master_low, BF16)
    whole_rows = share % LANES == 0
    if whole_rows:
        routed = routed.reshape(-1, share // LANES, LANES)
    own = lax.all_to_all(routed, ("fsdp", "tp"), split_axis=0, concat_axis=0, tiled=True)

    def local_weights(l):
        return {
            "qkv": jnp.concatenate([query_w[l], key_w[l], value_w[l]], axis=1),
            "o": out_w[l].T,
            "g": gate_w[l],
            "u": up_w[l],
            "d": down_w[l].T,
        }

    local = [local_weights(l) for l in range(LAYERS)]
    first_names = [(0, "qkv"), (0, "o"), (0, "g"), (0, "u"), (0, "d"), (1, "qkv"), (1, "o"), (1, "g")]
    late = jnp.concatenate([local[1]["u"], local[1]["d"]], axis=1)
    arrays = [local[l][name] for l, name in first_names]
    if fsdp_count == 16:
        part = hidden_cols * 4 // 9 // LANES * LANES
        plan = [
            ("zxy", 0, (0, arrays[0].shape[1])), ("zxy", 1, (0, arrays[1].shape[1])),
            ("zyx", 5, (0, arrays[5].shape[1])), ("zyx", 6, (0, arrays[6].shape[1])),
            ("zxy", 2, (0, hidden_cols)), ("zyx", 3, (0, hidden_cols)),
            ("xyz", 4, (part, hidden_cols - part)), ("yxz", 7, (part, hidden_cols - part)),
            ("zxy", 4, (0, part)), ("zyx", 7, (0, part)),
        ]
        first = gather_weights(arrays, plan, fsdp_count, 11)
    else:
        first = [lax.all_gather(a, "fsdp", axis=0, tiled=True) for a in arrays]
    own, late, first = lax.optimization_barrier((own, late, first))
    late_all = lax.all_gather(late, "fsdp", axis=0, tiled=True)

    if whole_rows:
        own_rows = own.reshape(-1, LANES)
    else:
        own_rows = own.reshape(-1).reshape(-1, LANES)
    layer_rows = sum(n for _, n in PIECES) * RANK // LANES

    def unpack(l):
        at = l * layer_rows
        got = {}
        for name, n in PIECES:
            count = n * RANK // LANES
            rows = own_rows[at : at + count]
            at += count
            if name in ("Eo", "Ed"):
                rows = lax.dynamic_slice_in_dim(rows, tp_place * (count // tp_count), count // tp_count, 0)
            if name[0] == "X":
                if name in ("Xq", "Xg", "Xu"):
                    parts = n // LANES
                    rows = rows.reshape(RANK, parts, LANES)
                    rows = lax.dynamic_slice_in_dim(
                        rows, tp_place * (parts // tp_count), parts // tp_count, 1
                    )
                got[name] = rows.reshape(RANK, -1)
            else:
                got[name] = expand_entry(rows)
        return got

    maps, spares = [], []
    for l in range(LAYERS):
        m = unpack(l)
        m["enter_qkv"] = dot(
            jnp.concatenate([m["Eq"], m["Ek"], m["Ev"]], axis=1),
            jnp.concatenate([slot_pick(i) for i in range(3)], axis=0), BF16,
        )
        m["enter_gu"] = dot(
            jnp.concatenate([m["Eg"], m["Eu"]], axis=1),
            jnp.concatenate([slot_pick(i) for i in range(2)], axis=0), BF16,
        )
        m["leave_o"] = in_slot(ADAPTER_SCALING * m["Xo"], 0)
        m["leave_d"] = in_slot(ADAPTER_SCALING * m["Xd"], 0)
        spares.append({
            "qkv": ADAPTER_SCALING * jnp.concatenate(
                [in_slot(m["Xq"], 0), in_slot(m["Xk"], 1), in_slot(m["Xv"], 2)], axis=1
            ),
            "o": dot_tn(slot_pick(0), m["Eo"].T, BF16),
            "g": ADAPTER_SCALING * in_slot(m["Xg"], 0),
            "u": ADAPTER_SCALING * in_slot(m["Xu"], 1),
            "d": dot_tn(slot_pick(0), m["Ed"].T, BF16),
        })
        maps.append(m)

    weights = [dict(), dict()]
    for (l, name), array in zip(first_names, first):
        weights[l][name] = (array, spares[l][name].astype(BF16))
    weights[1]["u"] = (late_all, spares[1]["u"].astype(BF16))
    weights[1]["d"] = (late_all, spares[1]["d"].astype(BF16))
    ffn_weights = [w["g"] + w["u"] + w["d"] for w in weights]
    ffn_offsets = [(0, 0, 0), (0, 0, hidden_cols)]
    cosine, sine = rope_tables(positions)
    gains = norm_gains.astype(F32)
    heads = head_gains.astype(F32)

    def gain(l, i):
        return gains[l, i][None, :]

    kept = []
    normed = exchange(body_enter, 1, "enter", None, [hidden_in], [gain(0, 0)], [], True)[0]
    x = hidden_in
    for l in range(LAYERS):
        w = weights[l]
        r = {"x": x, "normed": normed}
        m = maps[l]
        (
            r["raw"], r["qkv"], r["attn"], r["mid_qkv"], r["mid_o"], r["stats"], share_o,
        ) = attention_forward(
            normed, m["enter_qkv"], m["leave_o"], heads[l], cosine, sine, segments, w["qkv"],
            w["o"], scale,
        )
        r["attn_branch"], r["middle"], r["normed_two"] = exchange(
            body_middle, 2 if l == 0 else 3, "middle", share_o, [x], [gain(l, 1), gain(l, 2)],
            [F32, F32], True,
        )
        r["gelu"], r["slope"], r["hidden"], r["mid_gu"], r["mid_d"], share_f = ffn_forward(
            r["normed_two"], m["enter_gu"], m["leave_d"], ffn_weights[l], ffn_offsets[l]
        )
        if l + 1 < LAYERS:
            r["ffn_branch"], x, normed = exchange(
                body_next, 4, "next", share_f, [r["middle"]], [gain(l, 3), gain(l + 1, 0)],
                [F32, F32], True,
            )
        else:
            result, grad_ffn = exchange(
                body_turn, 5, "turn", share_f, [r["middle"], out_grad], [gain(l, 3)], [BF16], True
            )
        kept.append(r)

    grad_out = out_grad
    layer_grads = [None] * LAYERS
    for l in reversed(range(LAYERS)):
        w, r, m = weights[l], kept[l], maps[l]
        pieces = {}

        share_n2, pieces["Xg"], pieces["Xu"], pieces["Ed"], pieces["Xd"], entry_gu = ffn_backward(
            grad_ffn, r["normed_two"], m["enter_gu"], m["leave_d"], r, ffn_weights[l], ffn_offsets[l]
        )
        pieces["Eg"], pieces["Eu"] = entry_gu[:, :LANES], entry_gu[:, LANES:]
        grad_middle, grad_branch = exchange(
            body_back_middle, 6 if l == 1 else 7, "back_middle", share_n2,
            [grad_out, r["middle"], r["attn_branch"]], [gain(l, 2), gain(l, 1)], [F32], True,
        )
        share_n, entry_qkv, pieces["Eo"], exit_qkv, pieces["Xo"] = attention_backward(
            grad_branch, m["enter_qkv"], m["leave_o"], heads[l], cosine, sine, segments, r, w["qkv"],
            w["o"], scale,
        )
        for i, name in enumerate("qkv"):
            pieces["E" + name] = entry_qkv[:, i * LANES : (i + 1) * LANES]
        pieces["Xq"] = exit_qkv[:, :head_cols]
        pieces["Xk"] = exit_qkv[:, head_cols : head_cols + HD]
        pieces["Xv"] = exit_qkv[:, head_cols + HD :]
        if l > 0:
            grad_out, grad_ffn = exchange(
                body_back_next, 8, "back_next", share_n,
                [grad_middle, r["x"], kept[l - 1]["ffn_branch"]], [gain(l, 0), gain(l - 1, 3)],
                [F32], True,
            )
        else:
            grad_out = exchange(
                body_back_last, 9, "back_last", share_n, [grad_middle, r["x"]], [gain(l, 0)], [F32], False
            )[0]
        rows = []
        for name, n in PIECES:
            piece = pieces[name]
            if name in ("Eo", "Ed"):
                piece = lax.dynamic_update_slice_in_dim(
                    jnp.zeros((n * RANK // LANES, LANES), BF16), piece, tp_place * piece.shape[0], 0
                )
            if name in ("Xq", "Xg", "Xu"):
                piece = lax.dynamic_update_slice_in_dim(
                    jnp.zeros((RANK, n), BF16), piece, tp_place * piece.shape[1], 1
                )
            rows.append(piece.reshape(-1, LANES))
        layer_grads[l] = rows

    flat = jnp.concatenate(layer_grads[0] + layer_grads[1], axis=0)
    if whole_rows:
        flat = flat.reshape(fsdp_count * tp_count, share // LANES, LANES)
    else:
        flat = flat.reshape(-1).reshape(fsdp_count * tp_count, 1, share)
    chip_sum = pair_sum(flat, 10)
    arrived = lax.all_to_all(chip_sum, "fsdp", split_axis=0, concat_axis=0, tiled=True).reshape(fsdp_count, share)
    owner_pick = (set_range[:, None] == set_ids[None, :]).astype(BF16)
    set_grads = dot(owner_pick, arrived)
    first_new = BETA_ONE * first_moment + (1.0 - BETA_ONE) * set_grads
    second_new = BETA_TWO * second_moment + (1.0 - BETA_TWO) * set_grads * set_grads
    first_hat = first_new / (1.0 - BETA_ONE**ADAM_STEPS)
    second_hat = second_new / (1.0 - BETA_TWO**ADAM_STEPS)
    new_master = adapters - LEARN_RATE * (
        first_hat / (jnp.sqrt(second_hat) + ADAM_EPS) + DECAY_RATE * adapters
    )
    return (
        result, grad_out, set_grads, new_master, first_new, second_new, new_master.astype(BF16),
    )


def solution(mesh):
    return jax.shard_map(
        shards,
        mesh=mesh,
        in_specs=(
            P(("fsdp", "tp"), None),
            P(("fsdp", "tp"), None),
            P("fsdp"),
            P("fsdp"),
            P(),
            P(None, "fsdp", "tp"),
            P(None, "fsdp", None),
            P(None, "fsdp", None),
            P(None, "tp", "fsdp"),
            P(None, "fsdp", "tp"),
            P(None, "fsdp", "tp"),
            P(None, "tp", "fsdp"),
            P(),
            P(),
            P(None, ("fsdp", "tp")),
            P(None, ("fsdp", "tp")),
            P(None, ("fsdp", "tp")),
        ),
        out_specs=(
            P(("fsdp", "tp"), None),
            P(("fsdp", "tp"), None),
            P(None, ("fsdp", "tp")),
            P(None, ("fsdp", "tp")),
            P(None, ("fsdp", "tp")),
            P(None, ("fsdp", "tp")),
            P(None, ("fsdp", "tp")),
        ),
        check_vma=False,
    )
```

profile of v0, /device:TPU:0, one launch (start us, length us, event | category | flops | bytes accessed | tf_op | source)
XLA Modules:
  0.0 856.0 jit_solution(750193632535368073)
XLA Ops:
  11.9 7.3 all-to-all-start
  23.7 309.2 %gather_weights.1 = (bf16[1152,1024]{1,0:T(8,128)(2,1)}, bf16[1152,512]{1,0:T(8,128)(2,1)}, bf16[1152,3456]{1,0:T(8,128)(2,1)}, bf16[1152,3456]{1,0:T(8,128)(2,1...) custom-call(bf16[72,1024]{1,0:T(8,128)(2,1)} %get-tuple-element.252., ...), custom_call_target="tpu_custom_call" | custom-call | tf_op jit(solution)/shard_map/gather_weights/pallas_call | solution.py:277
  335.8 5.8 enter.1.normed
  365.6 18.3 %attention_forward.2 = (f32[1024,768]{1,0:T(8,128)}, bf16[1024,1024]{1,0:T(8,128)(2,1)}, bf16[1024,512]{1,0:T(8,128)(2,1)}, bf16[1024,128]{1,0:T(8,128)(2,1)}, b...) custom-call(bf16[1024,1152]{1,0:T(8,128)(2,1)} %enter.1.normed, ...), custom_call_target="tpu_custom_call" | custom-call | tf_op jit(solution)/shard_map/attention_forward/pallas_call | solution.py:520
  384.0 9.9 %middle.2 = (f32[512,1152]{1,0:T(8,128)}, f32[512,1152]{1,0:T(8,128)}, bf16[1024,1152]{1,0:T(8,128)(2,1)}) custom-call(bf16[1024,1152]{1,0:T(8,128)(2,1)} %get-tuple-element.101.refs_0_, bf16[512,1152]{1,0:T(8,128)(2,1)} %refs_2_.3, f32[1,1152]{1,0:T(1,128)} %get-tuple-element.225.refs_2_.refs_5_, f32[1,1152]{1,0:T(1,128)} %get-tuple-element.224.refs_3_.refs_4_), custom_call_target="tpu_custom_call" | custom-call | tf_op jit(solution)/shard_map/middle/pallas_call | solution.py:150
  399.8 46.3 %ffn_forward.2 = (bf16[1024,3456]{1,0:T(8,128)(2,1)}, bf16[1024,3456]{1,0:T(8,128)(2,1)}, bf16[1024,3456]{1,0:T(8,128)(2,1)}, bf16[1024,128]{1,0:T(8,128)(2,1)},...) custom-call(bf16[1024,1152]{1,0:T(8,128)(2,1)} %get-tuple-element.102.z, ...), custom_call_target="tpu_custom_call" | custom-call | tf_op jit(solution)/shard_map/ffn_forward/pallas_call | solution.py:758
  446.2 10.5 %next.1 = (f32[512,1152]{1,0:T(8,128)}, f32[512,1152]{1,0:T(8,128)}, bf16[1024,1152]{1,0:T(8,128)(2,1)}) custom-call(bf16[1024,1152]{1,0:T(8,128)(2,1)} %get-tuple-element.106.refs_0_, f32[512,1152]{1,0:T(8,128)} %get-tuple-element.107.refs_1_.refs_2_, f32[1,1152]{1,0:T(1,128)} %get-tuple-element.223.refs_2_.refs_5_, ...), custom_call_target="tpu_custom_call" | custom-call | tf_op jit(solution)/shard_map/next/pallas_call | solution.py:150
  459.9 18.3 %attention_forward.3 = (f32[1024,768]{1,0:T(8,128)}, bf16[1024,1024]{1,0:T(8,128)(2,1)}, bf16[1024,512]{1,0:T(8,128)(2,1)}, bf16[1024,128]{1,0:T(8,128)(2,1)}, b...) custom-call(bf16[1024,1152]{1,0:T(8,128)(2,1)} %get-tuple-element.108.normed, ...), custom_call_target="tpu_custom_call" | custom-call | tf_op jit(solution)/shard_map/attention_forward/pallas_call | solution.py:520
  478.3 10.2 %middle.3 = (f32[512,1152]{1,0:T(8,128)}, f32[512,1152]{1,0:T(8,128)}, bf16[1024,1152]{1,0:T(8,128)(2,1)}) custom-call(bf16[1024,1152]{1,0:T(8,128)(2,1)} %get-tuple-element.111.refs_0_, f32[512,1152]{1,0:T(8,128)} %get-tuple-element.112.refs_1_.refs_2_, f32[1,1152]{1,0:T(1,128)} %get-tuple-element.221.refs_2_.refs_5_, ...), custom_call_target="tpu_custom_call" | custom-call | tf_op jit(solution)/shard_map/middle/pallas_call | solution.py:150
  494.4 20.5 %all-gather.2.cloned.1.call-done.w_u.w_d = bf16[1152,6912]{1,0:T(8,128)(2,1)} async-done(((bf16[72,6912]{1,0:T(8,128)(2,1)}), bf16[1152,6912]{1,0:T(8,128)(2,1)}) %all-gather.2.cloned.1.call-update) | async-done | bytes 15925264 | tf_op jit(solution)/shard_map/all_gather | solution.py:929
  515.0 45.9 %ffn_forward.3 = (bf16[1024,3456]{1,0:T(8,128)(2,1)}, bf16[1024,3456]{1,0:T(8,128)(2,1)}, bf16[1024,3456]{1,0:T(8,128)(2,1)}, bf16[1024,128]{1,0:T(8,128)(2,1)},...) custom-call(bf16[1024,1152]{1,0:T(8,128)(2,1)} %get-tuple-element.113.z, ...), custom_call_target="tpu_custom_call" | custom-call | tf_op jit(solution)/shard_map/ffn_forward/pallas_call | solution.py:758
  560.9 9.4 %turn.1 = (bf16[512,1152]{1,0:T(8,128)(2,1)}, bf16[1024,1152]{1,0:T(8,128)(2,1)}) custom-call(bf16[1024,1152]{1,0:T(8,128)(2,1)} %get-tuple-element.116.refs_0_, f32[512,1152]{1,0:T(8,128)} %get-tuple-element.117.refs_1_.refs_2_, bf16[512,1152]{1,0:T(8,128)(2,1)} %refs_1_.3, f32[1,1152]{1,0:T(1,128)} %get-tuple-element.219.refs_3_), custom_call_target="tpu_custom_call" | custom-call | tf_op jit(solution)/shard_map/turn/pallas_call | solution.py:150
  570.3 66.5 %ffn_backward.2 = (bf16[1024,1152]{1,0:T(8,128)(2,1)}, bf16[16,3456]{1,0:T(8,128)(2,1)}, bf16[16,3456]{1,0:T(8,128)(2,1)}, bf16[432,128]{1,0:T(8,128)(2,1)}, bf1...) custom-call(bf16[1024,1152]{1,0:T(8,128)(2,1)} %get-tuple-element.119.grad, bf16[1024,1152]{1,0:T(8,128)(2,1)} %get-tuple-element.113.z, ...), custom_call_target="tpu_custom_call" | custom-call | tf_op jit(solution)/shard_map/ffn_backward/pallas_call | solution.py:850
  636.8 11.2 %back_middle.2 = (f32[512,1152]{1,0:T(8,128)}, bf16[1024,1152]{1,0:T(8,128)(2,1)}) custom-call(bf16[1024,1152]{1,0:T(8,128)(2,1)} %get-tuple-element.125.refs_0_, bf16[512,1152]{1,0:T(8,128)(2,1)} %refs_1_.3, f32[512,1152]{1,0:T(8,128)} %get-tuple-element.117.refs_1_.refs_2_, f32[512,1152]{1,0:T(8,128)} %get-tuple-element.126.refs_3_, ...), custom_call_target="tpu_custom_call" | custom-call | tf_op jit(solution)/shard_map/back_middle/pallas_call | solution.py:150
  648.0 30.4 %attention_backward.2 = (bf16[1024,1152]{1,0:T(8,128)(2,1)}, bf16[144,384]{1,0:T(8,128)(2,1)}, bf16[64,128]{1,0:T(8,128)(2,1)}, bf16[16,1024]{1,0:T(8,128)(2,1)}, bf16[16,1152]{1,0:T(8,128)(2,1)}) custom-call(bf16[1024,1152]{1,0:T(8,128)(2,1)} %get-tuple-element.127.grad_branch, bf16[1152,128]{1,0:T(8,128)(2,1)} %convolution_convert_fusion.4.enter, ...), custom_call_target="tpu_custom_call" | custom-call | tf_op jit(solution)/shard_map/attention_backward/pallas_call | solution.py:637
  678.4 11.2 %back_next.1 = (f32[512,1152]{1,0:T(8,128)}, bf16[1024,1152]{1,0:T(8,128)(2,1)}) custom-call(bf16[1024,1152]{1,0:T(8,128)(2,1)} %get-tuple-element.134.refs_0_, f32[512,1152]{1,0:T(8,128)} %get-tuple-element.135.refs_1_, f32[512,1152]{1,0:T(8,128)} %get-tuple-element.112.refs_1_.refs_2_, f32[512,1152]{1,0:T(8,128)} %get-tuple-element.136.refs_3_, ...), custom_call_target="tpu_custom_call" | custom-call | tf_op jit(solution)/shard_map/back_next/pallas_call | solution.py:150
  689.6 66.3 %ffn_backward.3 = (bf16[1024,1152]{1,0:T(8,128)(2,1)}, bf16[16,3456]{1,0:T(8,128)(2,1)}, bf16[16,3456]{1,0:T(8,128)(2,1)}, bf16[432,128]{1,0:T(8,128)(2,1)}, bf1...) custom-call(bf16[1024,1152]{1,0:T(8,128)(2,1)} %get-tuple-element.137.grad, bf16[1024,1152]{1,0:T(8,128)(2,1)} %get-tuple-element.102.z, ...), custom_call_target="tpu_custom_call" | custom-call | tf_op jit(solution)/shard_map/ffn_backward/pallas_call | solution.py:850
  756.0 11.6 %back_middle.3 = (f32[512,1152]{1,0:T(8,128)}, bf16[1024,1152]{1,0:T(8,128)(2,1)}) custom-call(bf16[1024,1152]{1,0:T(8,128)(2,1)} %get-tuple-element.143.refs_0_, f32[512,1152]{1,0:T(8,128)} %get-tuple-element.144.refs_1_, f32[512,1152]{1,0:T(8,128)} %get-tuple-element.107.refs_1_.refs_2_, f32[512,1152]{1,0:T(8,128)} %get-tuple-element.145.refs_3_, ...), custom_call_target="tpu_custom_call" | custom-call | tf_op jit(solution)/shard_map/back_middle/pallas_call | solution.py:150
  767.5 30.2 %attention_backward.3 = (bf16[1024,1152]{1,0:T(8,128)(2,1)}, bf16[144,384]{1,0:T(8,128)(2,1)}, bf16[64,128]{1,0:T(8,128)(2,1)}, bf16[16,1024]{1,0:T(8,128)(2,1)}, bf16[16,1152]{1,0:T(8,128)(2,1)}) custom-call(bf16[1024,1152]{1,0:T(8,128)(2,1)} %get-tuple-element.146.grad_branch, bf16[1152,128]{1,0:T(8,128)(2,1)} %convolution_convert_fusion.6.enter, ...), custom_call_target="tpu_custom_call" | custom-call | tf_op jit(solution)/shard_map/attention_backward/pallas_call | solution.py:637
  807.6 5.5 pair_sum.1
  813.1 3.8 all-to-all-start.1
  817.0 7.4 back_last.1
  824.4 16.6 %all-to-all-done.1 = bf16[16,245,128]{2,1,0:T(8,128)(2,1)S(1)} async-done(((bf16[16,245,128]{2,1,0:T(8,128)(2,1)}), bf16[16,245,128]{2,1,0:T(8,128)(2,1)S(1)}, u32[]{:S(2)}, u32[]{:S(2)}) %all-to-all-start.1) | async-done | bytes 1003552 | tf_op jit(solution)/shard_map/all_to_all | solution.py:1080
  841.0 4.2 fusion.126
  (292 shorter events, 63.3 us)
Async XLA Ops:
  11.9 322.1 %all-to-all-start = ((bf16[32,245,128]{2,1,0:T(8,128)(2,1)}), bf16[32,245,128]{2,1,0:T(8,128)(2,1)S(1)}, u32[]{:S(2)}, u32[]{:S(2)}) async-start(bf16[32,245,128]{2,1,0:T(8,128)(2,1)} %reshape.192), calls=%async_computation | async-start | bytes 4063232 | tf_op jit(solution)/shard_map/all_to_all | solution.py:901
  19.2 495.7 %all-gather.2.cloned.1.call-start = ((), (), s32[]{:S(2)}) async-start(), calls=%async_computation.2 | async-start | bytes 16920576 | tf_op jit(solution)/shard_map/all_gather | solution.py:929
  341.7 22.8 %copy-start.67 = (pred[512]{0:T(512)(128)(4,1)}, pred[512]{0:T(512)(128)(4,1)S(1)}, u32[]{:S(2)}) copy-start(pred[512]{0:T(512)(128)(4,1)S(1)} %fusion.117) | copy-start | bytes 1540
  341.7 53.3 %copy-start.61 = (s32[128]{0:T(128)}, s32[128]{0:T(128)S(1)}, u32[]{:S(2)}) copy-start(s32[128]{0:T(128)S(1)} %get-tuple-element.260) | copy-start | bytes 1540
  341.7 53.3 %copy-start.63 = (s32[128]{0:T(128)}, s32[128]{0:T(128)S(1)}, u32[]{:S(2)}) copy-start(s32[128]{0:T(128)S(1)} %get-tuple-element.261) | copy-start | bytes 1540
  341.7 53.3 %copy-start.49 = (pred[128]{0:T(512)(128)(4,1)}, pred[128]{0:T(512)(128)(4,1)S(1)}, u32[]{:S(2)}) copy-start(pred[128]{0:T(512)(128)(4,1)S(1)} %get-tuple-element.256) | copy-start | bytes 388
  341.7 53.3 %copy-start.65 = (pred[128]{0:T(512)(128)(4,1)}, pred[128]{0:T(512)(128)(4,1)S(1)}, u32[]{:S(2)}) copy-start(pred[128]{0:T(512)(128)(4,1)S(1)} %get-tuple-element.257) | copy-start | bytes 388
  341.7 53.2 %copy-start.51 = (s32[128]{0:T(128)}, s32[128]{0:T(128)S(1)}, u32[]{:S(2)}) copy-start(s32[128]{0:T(128)S(1)} %get-tuple-element.262) | copy-start | bytes 1540
  341.7 53.2 %copy-start.53 = (s32[128]{0:T(128)}, s32[128]{0:T(128)S(1)}, u32[]{:S(2)}) copy-start(s32[128]{0:T(128)S(1)} %get-tuple-element.263) | copy-start | bytes 1540
  341.8 22.7 %copy-start.57 = (s32[512]{0:T(512)}, s32[512]{0:T(512)S(1)}, u32[]{:S(2)}) copy-start(s32[512]{0:T(512)S(1)} %get-tuple-element.264) | copy-start | bytes 6148
  341.8 22.7 %copy-start.59 = (s32[512]{0:T(512)}, s32[512]{0:T(512)S(1)}, u32[]{:S(2)}) copy-start(s32[512]{0:T(512)S(1)} %get-tuple-element.265) | copy-start | bytes 6148
  341.8 53.2 %copy-start.47 = (pred[3456]{0:T(1024)(128)(4,1)}, pred[3456]{0:T(1024)(128)(4,1)S(1)}, u32[]{:S(2)}) copy-start(pred[3456]{0:T(1024)(128)(4,1)S(1)} %fusion.107) | copy-start | bytes 10372
  341.8 53.2 %copy-start.41 = (s32[3456]{0:T(1024)}, s32[3456]{0:T(1024)S(1)}, u32[]{:S(2)}) copy-start(s32[3456]{0:T(1024)S(1)} %get-tuple-element.266) | copy-start | bytes 41476
  341.9 53.2 %copy-start.43 = (s32[3456]{0:T(1024)}, s32[3456]{0:T(1024)S(1)}, u32[]{:S(2)}) copy-start(s32[3456]{0:T(1024)S(1)} %get-tuple-element.267) | copy-start | bytes 41476
  342.0 21.4 %copy-start.36 = (bf16[128,128]{1,0:T(8,128)(2,1)}, bf16[128,128]{1,0:T(8,128)(2,1)S(1)}, u32[]{:S(2)}) copy-start(bf16[128,128]{1,0:T(8,128)(2,1)S(1)} %get-tuple-element.249) | copy-start | bytes 98308
  342.0 51.9 %copy-start.32 = (bf16[128,128]{1,0:T(8,128)(2,1)}, bf16[128,128]{1,0:T(8,128)(2,1)S(1)}, u32[]{:S(2)}) copy-start(bf16[128,128]{1,0:T(8,128)(2,1)S(1)} %get-tuple-element.248) | copy-start | bytes 98308
  342.0 51.9 %copy-start.34 = (bf16[128,128]{1,0:T(8,128)(2,1)}, bf16[128,128]{1,0:T(8,128)(2,1)S(1)}, u32[]{:S(2)}) copy-start(bf16[128,128]{1,0:T(8,128)(2,1)S(1)} %get-tuple-element.250) | copy-start | bytes 98308
  446.1 11.4 %copy-start.12 = (bf16[1152,128]{1,0:T(8,128)(2,1)S(1)}, bf16[1152,128]{1,0:T(8,128)(2,1)}, u32[]{:S(2)}) copy-start(bf16[1152,128]{1,0:T(8,128)(2,1)} %get-tuple-element.236) | copy-start | bytes 884740
  767.5 35.0 %copy-start.21 = (bf16[16,3456]{1,0:T(8,128)(2,1)S(1)}, bf16[16,3456]{1,0:T(8,128)(2,1)}, u32[]{:S(2)}) copy-start(bf16[16,3456]{1,0:T(8,128)(2,1)} %get-tuple-element.160) | copy-start | bytes 331780
  767.5 36.2 %copy-start.27 = (bf16[144,256]{1,0:T(8,128)(2,1)S(1)}, bf16[144,256]{1,0:T(8,128)(2,1)}, u32[]{:S(2)}) copy-start(bf16[144,256]{1,0:T(8,128)(2,1)} %get-tuple-element.159) | copy-start | bytes 221188
  813.1 27.9 %all-to-all-start.1 = ((bf16[16,245,128]{2,1,0:T(8,128)(2,1)}), bf16[16,245,128]{2,1,0:T(8,128)(2,1)S(1)}, u32[]{:S(2)}, u32[]{:S(2)}) async-start(bf16[16,245,128]{2,1,0:T(8,128)(2,1)} %pair_sum.1), calls=%async_computation.1 | async-start | bytes 2031616 | tf_op jit(solution)/shard_map/all_to_all | solution.py:1080
  816.9 24.0 %copy-start.1 = (f32[8,31360]{1,0:T(8,128)S(1)}, f32[8,31360]{1,0:T(8,128)}, u32[]{:S(2)}) copy-start(f32[8,31360]{1,0:T(8,128)} %param.31) | copy-start | bytes 3010564
  816.9 24.0 %copy-start.3 = (f32[8,31360]{1,0:T(8,128)S(1)}, f32[8,31360]{1,0:T(8,128)}, u32[]{:S(2)}) copy-start(f32[8,31360]{1,0:T(8,128)} %param.32) | copy-start | bytes 3010564
  816.9 24.0 %copy-start.55 = (s32[16]{0:T(128)S(1)}, s32[16]{0:T(128)}, u32[]{:S(2)}) copy-start(s32[16]{0:T(128)} %param.21) | copy-start | bytes 196
  (48 other events, 255.3 us)
Sparse Core Ops, SparseCore 0:
  334.1 180.7 all-gather.1
where the time goes:
time: 863 us; the launch traced here: 856 us
  Pallas kernels  724 us (84%)
  waiting for transfers between devices  37.1 us (4%)
  local copies, waits for them, and re-layouts  33.6 us (4%)
  matrix products  18.3 us (2%)
  between operations  16.1 us (2%)
  other arithmetic  15.5 us (2%)
  starting transfers between devices  11.2 us (1%)
    pallas_call x1, Pallas kernels, gather_weights(): pl.pallas_call(functools.partial(gather_kernel, plan, nz, rows, len(array...  309 us
    pallas_call x2, Pallas kernels, ffn_backward(): pl.pallas_call(functools.partial(ffn_backward_kernel, offsets, steps), gr...  133 us
    pallas_call x2, Pallas kernels, ffn_forward(): pl.pallas_call(functools.partial(ffn_forward_kernel, offsets, steps), gri...  92.2 us
    pallas_call x9, Pallas kernels, exchange(): pl.pallas_call(functools.partial(exchange_kernel, body, partial is not No...  87.3 us
    pallas_call x2, Pallas kernels, attention_backward(): pl.pallas_call(functools.partial(attention_backward_kernel, local_heads,...  60.6 us
    pallas_call x2, Pallas kernels, attention_forward(): pl.pallas_call(functools.partial(attention_forward_kernel, local_heads, s...  36.7 us
    all_gather x1, waiting for transfers between devices, shards(): late_all = lax.all_gather(late, 'fsdp', axis=0, tiled=True)  20.5 us
  transfers between devices with their start and end apart: 3, of which 2 were waited for; matrix products, arithmetic and copies ran while one was open for 5% of the time, Pallas kernels for 51%

commit v1 on v0

--- a/solution.py
+++ b/solution.py
@@ -31,6 +31,7 @@
 F32 = jnp.float32
 BF16 = jnp.bfloat16
 MESH = pl.DeviceIdType.MESH
+EXCHANGE_CHUNKS = 8
 
 PIECES = (
     ("Eq", D), ("Xq", HEADS * HD), ("Ek", D), ("Xk", HD), ("Ev", D), ("Xv", HD),
@@ -63,33 +64,54 @@
 
 def exchange_kernel(body, has_partial, n_rows, n_gains, n_outs, has_send, n_chunks, *refs):
     refs = list(refs)
-    partial = refs.pop(0) if has_partial else None
-    rows = [refs.pop(0) for _ in range(n_rows)]
-    gains = [refs.pop(0) for _ in range(n_gains)]
-    outs = [refs.pop(0) for _ in range(n_outs)]
-    gathered = refs.pop(0) if has_send else None
+
+    def take(count):
+        out = refs[:count]
+        del refs[:count]
+        return out
+
+    partial = take(1)[0] if has_partial else None
+    rows, gains, outs = take(n_rows), take(n_gains), take(n_outs)
+    gathered = take(1)[0] if has_send else None
+    rows_here, outs_here = take(n_rows), take(n_outs)
+    row_sems, out_sems = take(2)
     if has_partial:
-        arrived, send_a, recv_a = refs[:3]
-        refs = refs[3:]
+        mine, arrived, mine_sems, send_a, recv_a = take(5)
     if has_send:
-        send_b, recv_b = refs[:2]
+        spread_here, keep_sems, send_b, recv_b = take(4)
     me = lax.axis_index("tp")
     other = 1 - me
+    half = (partial if has_partial else gathered).shape[0] // 2
+    chunk = half // n_chunks
+
+    def span(base, c):
+        return pl.ds(pl.multiple_of(base * half + c * chunk, chunk), chunk)
+
+    def local(c):
+        return pl.ds(c * chunk, chunk)
+
+    loads = []
+    for c in range(n_chunks):
+        group = [
+            pltpu.make_async_copy(r.at[local(c)], h.at[local(c)], row_sems.at[i, c])
+            for i, (r, h) in enumerate(zip(rows, rows_here))
+        ]
+        if has_partial:
+            group.append(
+                pltpu.make_async_copy(partial.at[span(me, c)], mine.at[local(c)], mine_sems.at[c])
+            )
+        for copy in group:
+            copy.start()
+        loads.append(group)
     barrier = pltpu.get_barrier_semaphore()
     pl.semaphore_signal(barrier, inc=1, device_id={"tp": other}, device_id_type=MESH)
     pl.semaphore_wait(barrier, 1)
-    half = (partial if has_partial else gathered).shape[0] // 2
-    chunk = half // n_chunks
-
-    def span(base, c):
-        return pl.ds(pl.multiple_of(base * half + c * chunk, chunk), chunk)
-
-    sends = []
+    sends, spreads, stores = [], [], []
     if has_partial:
         for c in range(n_chunks):
             copy = pltpu.make_async_remote_copy(
                 src_ref=partial.at[span(other, c)],
-                dst_ref=arrived.at[pl.ds(c * chunk, chunk)],
+                dst_ref=arrived.at[local(c)],
                 send_sem=send_a.at[c],
                 recv_sem=recv_a.at[c],
                 device_id={"tp": other},
@@ -98,21 +120,33 @@
             copy.start()
             sends.append(copy)
     gain_values = [g[...].astype(F32) for g in gains]
-    spreads = []
+
+    def release(c):
+        if has_send:
+            spreads[c].start()
+        for copy in stores[c]:
+            copy.start()
+
     for c in range(n_chunks):
-        local = pl.ds(c * chunk, chunk)
+        for copy in loads[c]:
+            copy.wait()
         total = None
         if has_partial:
             sends[c].wait_recv()
-            total = partial[span(me, c), :].astype(F32) + arrived[local, :].astype(F32)
-        values, spread = body(total, [r[local, :].astype(F32) for r in rows], gain_values)
-        for ref, value in zip(outs, values):
-            ref[local, :] = value.astype(ref.dtype)
+            total = mine[local(c), :].astype(F32) + arrived[local(c), :].astype(F32)
+        values, spread = body(total, [r[local(c), :].astype(F32) for r in rows_here], gain_values)
+        group = []
+        for i, (ref, here, value) in enumerate(zip(outs, outs_here, values)):
+            here[local(c), :] = value.astype(here.dtype)
+            group.append(pltpu.make_async_copy(here.at[local(c)], ref.at[local(c)], out_sems.at[i, c]))
         if has_send:
-            gathered[span(me, c), :] = spread.astype(BF16)
+            spread_here[local(c), :] = spread.astype(BF16)
+            group.append(
+                pltpu.make_async_copy(spread_here.at[local(c)], gathered.at[span(me, c)], keep_sems.at[c])
+            )
             spreads.append(
                 pltpu.make_async_remote_copy(
-                    src_ref=gathered.at[span(me, c)],
+                    src_ref=spread_here.at[local(c)],
                     dst_ref=gathered.at[span(me, c)],
                     send_sem=send_b.at[c],
                     recv_sem=recv_b.at[c],
@@ -120,45 +154,49 @@
                     device_id_type=MESH,
                 )
             )
-            if c > 0:
-                spreads[c - 1].start()
-    if has_send:
-        spreads[-1].start()
+        stores.append(group)
+        if c > 0:
+            release(c - 1)
+    release(n_chunks - 1)
     for copy in sends:
         copy.wait_send()
+    for c in range(n_chunks):
+        for copy in stores[c]:
+            copy.wait()
     for copy in spreads:
         copy.wait()
 
 
-def exchange(body, collective_id, name, partial, rows, gains, out_types, has_send, n_chunks=4):
-    operands = ([] if partial is None else [partial]) + list(rows) + list(gains)
+def exchange(body, collective_id, name, partial, rows, gains, out_types, has_send, n_chunks=EXCHANGE_CHUNKS):
+    operands = ([] if partial is None else [partial]) + list(rows)
     width = operands[0].shape[1]
     half = partial.shape[0] // 2 if partial is not None else rows[0].shape[0]
     outs = [jax.ShapeDtypeStruct((half, width), kind) for kind in out_types]
+    scratch = [pltpu.VMEM((half, width), r.dtype) for r in rows]
+    scratch += [pltpu.VMEM((half, width), kind) for kind in out_types]
+    scratch += [
+        pltpu.SemaphoreType.DMA((len(rows), n_chunks)),
+        pltpu.SemaphoreType.DMA((max(len(outs), 1), n_chunks)),
+    ]
+    each = pltpu.SemaphoreType.DMA((n_chunks,))
+    if partial is not None:
+        scratch += [pltpu.VMEM((half, width), partial.dtype)] * 2 + [each] * 3
     if has_send:
         outs.append(jax.ShapeDtypeStruct((2 * half, width), BF16))
-    scratch = []
-    if partial is not None:
-        scratch += [
-            pltpu.VMEM((half, width), partial.dtype),
-            pltpu.SemaphoreType.DMA((n_chunks,)),
-            pltpu.SemaphoreType.DMA((n_chunks,)),
-        ]
-    if has_send:
-        scratch += [pltpu.SemaphoreType.DMA((n_chunks,)), pltpu.SemaphoreType.DMA((n_chunks,))]
-    vmem = pl.BlockSpec(memory_space=pltpu.VMEM)
+        scratch += [pltpu.VMEM((half, width), BF16)] + [each] * 3
+    hbm = pl.BlockSpec(memory_space=pl.ANY)
     return pl.pallas_call(
         functools.partial(
             exchange_kernel, body, partial is not None, len(rows), len(gains), len(out_types),
             has_send, n_chunks,
         ),
         out_shape=outs,
-        in_specs=[vmem] * len(operands),
-        out_specs=[vmem] * len(outs),
+        in_specs=[hbm] * len(operands) + [pl.BlockSpec(memory_space=pltpu.VMEM)] * len(gains),
+        out_specs=[hbm] * len(outs),
         scratch_shapes=scratch,
         compiler_params=pltpu.CompilerParams(collective_id=collective_id, has_side_effects=True),
         name=name,
-    )(*operands)
+    )(*operands, *gains)
 
 
 def gather_kernel(plan, nz, rows, n_arrays, *refs):
@@ -331,6 +369,41 @@
     )(partial)
 
 
+def pair_gather_kernel(count, mine, both, send_sem, recv_sem, local_sem):
+    me = lax.axis_index("tp")
+    other = 1 - me
+    barrier = pltpu.get_barrier_semaphore()
+    pl.semaphore_signal(barrier, inc=1, device_id={"tp": other}, device_id_type=MESH)
+    pl.semaphore_wait(barrier, 1)
+    copies = []
+    for i in range(count):
+        place = both.at[2 * i + me]
+        copies.append(
+            pltpu.make_async_remote_copy(
+                src_ref=mine.at[i], dst_ref=place, send_sem=send_sem.at[i], recv_sem=recv_sem.at[i],
+                device_id={"tp": other}, device_id_type=MESH,
+            )
+        )
+        copies.append(pltpu.make_async_copy(mine.at[i], place, local_sem.at[i]))
+    for copy in copies:
+        copy.start()
+    for copy in copies:
+        copy.wait()
+
+
+def pair_gather(mine, collective_id):
+    count = mine.shape[0]
+    return pl.pallas_call(
+        functools.partial(pair_gather_kernel, count),
+        out_shape=jax.ShapeDtypeStruct((2 * count,) + mine.shape[1:], mine.dtype),
+        in_specs=[pl.BlockSpec(memory_space=pltpu.VMEM)],
+        out_specs=pl.BlockSpec(memory_space=pl.ANY),
+        scratch_shapes=[pltpu.SemaphoreType.DMA((count,))] * 3,
+        compiler_params=pltpu.CompilerParams(collective_id=collective_id, has_side_effects=True),
+        name="pair_gather",
+    )(mine)
+
+
 def body_enter(total, rows, gains):
     return [], rms(rows[0], gains[0])
 
@@ -362,34 +435,12 @@
 
 def body_back_last(total, rows, gains):
     return [rows[0] + rms_back(rows[1], gains[0], total)], None
-
-
-def lane_group_mask(count):
-    row = lax.broadcasted_iota(jnp.int32, (count, LANES), 0)
-    lane = lax.broadcasted_iota(jnp.int32, (count, LANES), 1)
-    return (lane // RANK) == (row % GROUPS)
-
-
-def expand_entry(flat_rows):
-    count = flat_rows.shape[0] * GROUPS
-    spread = jnp.broadcast_to(flat_rows[:, None, :], (flat_rows.shape[0], GROUPS, LANES))
-    return jnp.where(lane_group_mask(count), spread.reshape(count, LANES), 0).astype(BF16)
-
-
-def slot_pick(slot):
-    row = lax.broadcasted_iota(jnp.int32, (LANES, LANES), 0)
-    lane = lax.broadcasted_iota(jnp.int32, (LANES, LANES), 1)
-    return (lane == slot * RANK + row % RANK).astype(BF16)
 
 
 def slot_spread(slot):
     row = lax.broadcasted_iota(jnp.int32, (LANES, LANES), 0)
     lane = lax.broadcasted_iota(jnp.int32, (LANES, LANES), 1)
     return (row == slot * RANK + lane % RANK).astype(BF16)
-
-
-def in_slot(rows, slot):
-    return jnp.pad(rows, ((slot * RANK, LANES - (slot + 1) * RANK), (0, 0)))
 
 
 def rope_tables(positions):
@@ -538,18 +589,21 @@
 
 
 def attention_backward_kernel(
-    local_heads, scale, grad_branch, enter, leave, gains, cosine, sine, segment_column, segment_row,
-    spread, raw, qkv, attn, stats, normed, mid_qkv, mid_o, w_qkv, w_o, s_qkv, s_o,
-    share, entry_qkv, entry_o, exit_qkv, exit_o,
-    w_qkv_here, w_o_here, grad_attn, grad_raw, grad_k, grad_v, spread_qkv, spread_o, sems,
+    local_heads, scale, grad_branch, enter, leave, gains, segment_column, segment_row, spread, *refs
 ):
+    distant, refs = refs[:9], refs[9:]
+    w_qkv, w_o, s_qkv, s_o, share, entry_qkv, entry_o, exit_qkv, exit_o = refs[:9]
+    w_qkv_here, w_o_here, grad_attn, grad_raw, grad_k, grad_v, spread_qkv, spread_o, sems = refs[9:18]
+    near, near_sems = refs[18:27], refs[27]
+    loads = [pltpu.make_async_copy(*pair, near_sems.at[i]) for i, pair in enumerate(zip(distant, near))]
+    qkv, stats, raw, cosine, sine, normed, attn, mid_qkv, mid_o = near
     copies = [
         weight_copies((w_o, s_o), w_o_here, sems.at[0]),
         weight_copies((w_qkv, s_qkv), w_qkv_here, sems.at[1]),
     ]
-    for c in copies[0] + copies[1]:
+    for c in copies[0] + loads[:5] + copies[1] + loads[5:]:
         c.start()
-    blocks = normed.shape[0] // ROW_BLOCK
+    blocks = grad_branch.shape[0] // ROW_BLOCK
     key_col = local_heads * HD
     value_col = key_col + HD
     grad_k[...] = jnp.zeros_like(grad_k)
@@ -564,6 +618,9 @@
         mid = dot_nt(g, leave[...], BF16)
         spread_o[rows, :] = dot(mid, spread[:, :LANES], BF16)
         grad_attn[rows, :] = dot(jnp.concatenate([g, mid], axis=1), w_o_here[...], BF16)
+
+    for c in loads[:5]:
+        c.wait()
 
     @pl.loop(0, blocks)
     def _(i):
@@ -604,6 +661,9 @@
         spread_qkv[rows, :] = dot(mid, spread[...], BF16)
         share[rows, :] = (both[:, :-LANES] + dot_nt(mid, enter[...])).astype(BF16)
 
+    for c in loads[5:]:
+        c.wait()
+
     @pl.loop(0, normed.shape[1] // LANES)
     def _(j):
         wide = dot_tn(normed[:, rows_at(j, LANES)], spread_qkv[...])
@@ -629,6 +689,10 @@
     columns = w_qkv.shape[1]
     local_heads = columns // HD - 2
     spread = jnp.concatenate([slot_spread(i) for i in range(3)], axis=1)
+    distant = [
+        kept["qkv"], kept["stats"], kept["raw"], cosine, sine, kept["normed"], kept["attn"],
+        kept["mid_qkv"], kept["mid_o"],
+    ]
     shapes = [
         (length, width), (width // GROUPS, 3 * LANES), (local_heads * HD // GROUPS, LANES),
         (RANK, columns), (RANK, width),
@@ -637,7 +701,7 @@
     return pl.pallas_call(
         functools.partial(attention_backward_kernel, local_heads, scale),
         out_shape=[jax.ShapeDtypeStruct(shape, BF16) for shape in shapes],
-        in_specs=[vmem] * 16 + [pl.BlockSpec(memory_space=pl.ANY)] * 4,
+        in_specs=[vmem] * 7 + [pl.BlockSpec(memory_space=pl.ANY)] * 13,
         out_specs=[vmem] * len(shapes),
         scratch_shapes=[
             with_slots(w_qkv), with_slots(w_o),
@@ -645,12 +709,13 @@
             pltpu.VMEM((length, HD), F32), pltpu.VMEM((length, HD), F32),
             pltpu.VMEM((length, 3 * LANES), BF16), pltpu.VMEM((length, LANES), BF16),
             pltpu.SemaphoreType.DMA((2, 2)),
-        ],
+        ]
+        + [pltpu.VMEM(a.shape, a.dtype) for a in distant]
+        + [pltpu.SemaphoreType.DMA((len(distant),))],
         name="attention_backward",
     )(
-        grad_branch, enter, leave, gains, cosine, sine, segments[:, None], segments[None, :], spread,
-        kept["raw"], kept["qkv"], kept["attn"], kept["stats"], kept["normed"], kept["mid_qkv"],
-        kept["mid_o"], w_qkv, w_o, qkv_parts[1], o_parts[1],
+        grad_branch, enter, leave, gains, segments[:, None], segments[None, :], spread, *distant,
+        w_qkv, w_o, qkv_parts[1], o_parts[1],
     )
 
 
@@ -662,53 +727,79 @@
     return value, slope
 
 
-FFN_BLOCK = 1152
-
-
-def ffn_fetch(weights, offsets, buffers, sems, j, slot):
-    out = []
-    for k in range(3):
-        source, slots = weights[2 * k], weights[2 * k + 1]
-        here = buffers.at[k, slot]
-        start = pl.multiple_of(j * FFN_BLOCK, LANES)
-        rows = source.shape[0]
-        out.append(pltpu.make_async_copy(
-            source.at[:, pl.ds(offsets[k] + start, FFN_BLOCK)], here.at[pl.ds(0, rows)], sems.at[k, slot, 0]
-        ))
-        out.append(pltpu.make_async_copy(
-            slots.at[:, pl.ds(start, FFN_BLOCK)], here.at[pl.ds(rows, LANES)], sems.at[k, slot, 1]
-        ))
-    return out
-
-
-def ffn_step(weights, offsets, buffers, sems, steps):
+FFN_BLOCK = 1280
+
+
+def ffn_fetch(weights, offsets, buffers, sems, k, j, slot, count):
+    source, slots = weights[2 * k], weights[2 * k + 1]
+    start = pl.multiple_of(j * FFN_BLOCK, LANES)
+    rows = source.shape[0]
+    here = buffers.at[k, slot]
+    return [
+        pltpu.make_async_copy(
+            source.at[:, pl.ds(offsets[k] + start, count)],
+            here.at[pl.ds(0, rows), pl.ds(0, count)],
+            sems.at[k, slot, 0],
+        ),
+        pltpu.make_async_copy(
+            slots.at[:, pl.ds(start, count)],
+            here.at[pl.ds(rows, LANES), pl.ds(0, count)],
+            sems.at[k, slot, 1],
+        ),
+    ]
+
+
+def ffn_start(weights, offsets, buffers, sems, order, columns):
     j = pl.program_id(0)
-    slot = j % 2
+    steps = pl.cdiv(columns, FFN_BLOCK)
+
+    def start(step, slot, count):
+        for k in order:
+            for c in ffn_fetch(weights, offsets, buffers, sems, k, step, slot, count):
+                c.start()
 
     @pl.when(j == 0)
     def _():
-        for c in ffn_fetch(weights, offsets, buffers, sems, 0, 0):
-            c.start()
-
-    for c in ffn_fetch(weights, offsets, buffers, sems, j, slot):
-        c.wait()
-
-    @pl.when(j + 1 < steps)
+        start(0, 0, FFN_BLOCK)
+
+    @pl.when(j + 1 < steps - 1)
     def _():
-        for c in ffn_fetch(weights, offsets, buffers, sems, j + 1, 1 - slot):
-            c.start()
-
-    return slot
+        start(j + 1, 1 - j % 2, FFN_BLOCK)
+
+    @pl.when(j + 1 == steps - 1)
+    def _():
+        start(j + 1, 1 - j % 2, columns - (steps - 1) * FFN_BLOCK)
+
+
+def by_width(columns, step):
+    steps = pl.cdiv(columns, FFN_BLOCK)
+    last = pl.program_id(0) == steps - 1
+    pl.when(jnp.logical_not(last))(functools.partial(step, FFN_BLOCK))
+    pl.when(last)(functools.partial(step, columns - (steps - 1) * FFN_BLOCK))
+
+
+def add_to(total, part):
+    j = pl.program_id(0)
+
+    @pl.when(j == 0)
+    def _():
+        total[...] = part
+
+    @pl.when(j > 0)
+    def _():
+        total[...] += part
 
 
 def ffn_forward_kernel(
-    offsets, steps, z, enter, leave, w_g, s_g, w_u, s_u, w_d, s_d,
+    offsets, columns, z, enter, leave, w_g, s_g, w_u, s_u, w_d, s_d,
     gelu, slope, hidden, mid_gu, mid_d, share, buffers, joined, total, sems,
 ):
     j = pl.program_id(0)
+    slot = j % 2
     width = z.shape[1]
     blocks = z.shape[0] // ROW_BLOCK
-    slot = ffn_step((w_g, s_g, w_u, s_u, w_d, s_d), offsets, buffers, sems, steps)
+    weights = (w_g, s_g, w_u, s_u, w_d, s_d)
+    ffn_start(weights, offsets, buffers, sems, (0, 1, 2), columns)
 
     @pl.when(j == 0)
     def _():
@@ -717,27 +808,30 @@
         joined[:, :width] = z[...]
         joined[:, width:] = mid
 
-    @pl.loop(0, blocks)
-    def _(i):
-        rows = rows_at(i)
-        gate_pre = dot(joined[rows, :], buffers[0, slot])
-        up_pre = dot(joined[rows, :], buffers[1, slot])
-        value, rate = gelu_parts(gate_pre)
-        gelu[rows, :] = value.astype(BF16)
-        slope[rows, :] = (rate * up_pre).astype(BF16)
-        hidden[rows, :] = (value * up_pre).astype(BF16)
-
-    part = dot_nt(hidden[...], buffers[2, slot])
-
-    @pl.when(j == 0)
-    def _():
-        total[...] = part
-
-    @pl.when(j > 0)
-    def _():
-        total[...] += part
-
-    @pl.when(j == steps - 1)
+    def step(count):
+        def wait(k):
+            for c in ffn_fetch(weights, offsets, buffers, sems, k, j, slot, count):
+                c.wait()
+
+        wait(0)
+        wait(1)
+
+        @pl.loop(0, blocks)
+        def _(i):
+            rows = rows_at(i)
+            gate_pre = dot(joined[rows, :], buffers[0, slot, :, :count])
+            up_pre = dot(joined[rows, :], buffers[1, slot, :, :count])
+            value, rate = gelu_parts(gate_pre)
+            gelu[rows, :count] = value.astype(BF16)
+            slope[rows, :count] = (rate * up_pre).astype(BF16)
+            hidden[rows, :count] = (value * up_pre).astype(BF16)
+
+        wait(2)
+        add_to(total, dot_nt(hidden[:, :count], buffers[2, slot, :, :count]))
+
+    by_width(columns, step)
+
+    @pl.when(j == pl.num_programs(0) - 1)
     def _():
         mid = total[:, width:].astype(BF16)
         mid_d[...] = mid
@@ -747,7 +841,7 @@
 def ffn_forward(z, enter, leave, weights, offsets):
     length, width = z.shape
     columns = weights[1].shape[1]
-    steps = columns // FFN_BLOCK
+    steps = pl.cdiv(columns, FFN_BLOCK)
 
     def fixed(shape):
         return pl.BlockSpec(shape, lambda j: (0, 0), pipeline_mode=pl.Buffered(1))
@@ -756,7 +850,7 @@
     hbm = pl.BlockSpec(memory_space=pl.ANY)
     small = (length, LANES)
     return pl.pallas_call(
-        functools.partial(ffn_forward_kernel, offsets, steps),
+        functools.partial(ffn_forward_kernel, offsets, columns),
         grid=(steps,),
         out_shape=[jax.ShapeDtypeStruct((length, columns), BF16)] * 3
         + [jax.ShapeDtypeStruct(small, BF16)] * 2
@@ -775,15 +869,17 @@
 
 
 def ffn_backward_kernel(
-    offsets, steps, grad, z, enter, leave, mid_gu, mid_d, spread, gelu, slope, hidden,
+    offsets, columns, grad, z, enter, leave, mid_gu, mid_d, spread, gelu, slope, hidden,
     w_g, s_g, w_u, s_u, w_d, s_d,
     share, exit_g, exit_u, entry_d, exit_d, entry_gu,
     buffers, joined, grad_g, grad_u, total, spread_d, spread_gu, sems,
 ):
     j = pl.program_id(0)
+    slot = j % 2
     width = z.shape[1]
     blocks = z.shape[0] // ROW_BLOCK
-    slot = ffn_step((w_g, s_g, w_u, s_u, w_d, s_d), offsets, buffers, sems, steps)
+    weights = (w_g, s_g, w_u, s_u, w_d, s_d)
+    ffn_start(weights, offsets, buffers, sems, (2, 0, 1), columns)
 
     @pl.when(j == 0)
     def _():
@@ -793,32 +889,40 @@
         spread_d[...] = dot(mid, spread[:, :LANES], BF16)
         exit_d[...] = (ADAPTER_SCALING * dot_tn(mid_d[...], grad[...]))[:RANK].astype(BF16)
 
-    @pl.loop(0, blocks)
-    def _(i):
-        rows = rows_at(i)
-        grad_hidden = dot(joined[rows, :], buffers[2, slot])
-        grad_g[rows, :] = (grad_hidden * slope[rows, :].astype(F32)).astype(BF16)
-        grad_u[rows, :] = (grad_hidden * gelu[rows, :].astype(F32)).astype(BF16)
-
-    part = dot_nt(grad_g[...], buffers[0, slot]) + dot_nt(grad_u[...], buffers[1, slot])
-
-    @pl.when(j == 0)
-    def _():
-        total[...] = part
-
-    @pl.when(j > 0)
-    def _():
-        total[...] += part
-
-    exit_g[...] = (ADAPTER_SCALING * dot_tn(mid_gu[...], grad_g[...]))[:RANK].astype(BF16)
-    exit_u[...] = (ADAPTER_SCALING * dot_tn(mid_gu[...], grad_u[...]))[RANK : 2 * RANK].astype(BF16)
-
-    @pl.loop(0, FFN_BLOCK // LANES)
-    def _(i):
-        wide = dot_tn(hidden[:, rows_at(i, LANES)], spread_d[...])
-        entry_d[rows_at(i, RANK), :] = fold_rows(wide)
-
-    @pl.when(j == steps - 1)
+    def step(count):
+        def wait(k):
+            for c in ffn_fetch(weights, offsets, buffers, sems, k, j, slot, count):
+                c.wait()
+
+        wait(2)
+
+        @pl.loop(0, blocks)
+        def _(i):
+            rows = rows_at(i)
+            grad_hidden = dot(joined[rows, :], buffers[2, slot, :, :count])
+            grad_g[rows, :count] = (grad_hidden * slope[rows, :count].astype(F32)).astype(BF16)
+            grad_u[rows, :count] = (grad_hidden * gelu[rows, :count].astype(F32)).astype(BF16)
+
+        exit_g[:, :count] = (ADAPTER_SCALING * dot_tn(mid_gu[...], grad_g[:, :count]))[:RANK].astype(BF16)
+        exit_u[:, :count] = (ADAPTER_SCALING * dot_tn(mid_gu[...], grad_u[:, :count]))[
+            RANK : 2 * RANK
+        ].astype(BF16)
+        wait(0)
+        wait(1)
+        add_to(
+            total,
+            dot_nt(grad_g[:, :count], buffers[0, slot, :, :count])
+            + dot_nt(grad_u[:, :count], buffers[1, slot, :, :count]),
+        )
+
+        @pl.loop(0, count // LANES)
+        def _(i):
+            wide = dot_tn(hidden[:, rows_at(i, LANES)], spread_d[...])
+            entry_d[rows_at(i, RANK), :] = fold_rows(wide)
+
+    by_width(columns, step)
+
+    @pl.when(j == pl.num_programs(0) - 1)
     def _():
         mid = total[:, width:].astype(BF16)
         share[...] = (total[:, :width] + dot_nt(mid, enter[...])).astype(BF16)
@@ -833,7 +937,7 @@
 def ffn_backward(grad, z, enter, leave, kept, weights, offsets):
     length, width = z.shape
     columns = weights[1].shape[1]
-    steps = columns // FFN_BLOCK
+    steps = pl.cdiv(columns, FFN_BLOCK)
     spread = jnp.concatenate([slot_spread(i) for i in range(2)], axis=1)
 
     def fixed(shape):
@@ -848,7 +952,7 @@
     ]
     narrow = pl.BlockSpec((RANK, FFN_BLOCK), lambda j: (0, j))
     return pl.pallas_call(
-        functools.partial(ffn_backward_kernel, offsets, steps),
+        functools.partial(ffn_backward_kernel, offsets, columns),
         grid=(steps,),
         out_shape=[jax.ShapeDtypeStruct(shape, BF16) for shape in shapes],
         in_specs=[
@@ -878,6 +982,94 @@
     )
 
 
+def piece_starts(layer_idx):
+    starts, at = {}, layer_idx * sum(n for _, n in PIECES) * RANK // LANES
+    for name, n in PIECES:
+        starts[name] = at
+        at += n * RANK // LANES
+    return starts
+
+
+def unpack_kernel(head_cols, hidden_cols, rows, *refs):
+    outs, (values, tall) = refs[:-2], refs[-2:]
+    tp_place = lax.axis_index("tp")
+    sizes = dict(PIECES)
+
+    @pl.loop(0, rows.shape[0] // 16)
+    def _(i):
+        at = pl.ds(pl.multiple_of(i * 16, 16), 16)
+        values[at, :] = rows[at, :].astype(F32)
+
+    def entries(names, starts, count):
+        lane = lax.broadcasted_iota(jnp.int32, (count, LANES), 1)
+        for s in range(GROUPS):
+            row = jnp.zeros((count, LANES), F32)
+            for i, start in enumerate(starts):
+                moved = values[pl.ds(start, count), :]
+                if (i - s) % GROUPS:
+                    moved = pltpu.roll(moved, (i - s) % GROUPS * RANK, 1)
+                row = jnp.where(lane // RANK == i, moved, row)
+            tall[pl.ds(s, count, stride=GROUPS), :] = row
+
+    def exit_rows(out, start, stride, columns, slot, scale):
+        for j in range((columns.stop - columns.start) // LANES):
+            block = values[pl.ds(start + j, RANK, stride=stride), :] * scale
+            at = columns.start + j * LANES
+            out[slot * RANK : (slot + 1) * RANK, at : at + LANES] = block.astype(BF16)
+
+    for l in range(LAYERS):
+        starts = piece_starts(l)
+        enter_qkv, enter_gu, leave_o, leave_d, s_qkv, s_o, s_g, s_u, s_d = outs[9 * l : 9 * l + 9]
+        for out in (leave_o, leave_d, s_qkv, s_g, s_u):
+            out[...] = jnp.zeros_like(out)
+        for out, names in ((enter_qkv, ("Eq", "Ek", "Ev")), (enter_gu, ("Eg", "Eu"))):
+            entries(names, [starts[n] for n in names], D // GROUPS)
+            out[...] = tall[:D, :].astype(BF16)
+        for out, name, columns in ((s_o, "Eo", head_cols), (s_d, "Ed", hidden_cols)):
+            count = columns // GROUPS
+            entries((name,), [pl.multiple_of(starts[name] + tp_place * count, 8)], count)
+            for j in range(columns // LANES):
+                at = slice(j * LANES, (j + 1) * LANES)
+                out[:, at] = tall[at, :].T.astype(BF16)
+        exit_rows(leave_o, starts["Xo"], D // LANES, slice(0, D), 0, ADAPTER_SCALING)
+        exit_rows(leave_d, starts["Xd"], D // LANES, slice(0, D), 0, ADAPTER_SCALING)
+        for out, name, columns, slot in (
+            (s_qkv, "Xq", slice(0, head_cols), 0),
+            (s_qkv, "Xk", slice(head_cols, head_cols + HD), 1),
+            (s_qkv, "Xv", slice(head_cols + HD, head_cols + 2 * HD), 2),
+            (s_g, "Xg", slice(0, hidden_cols), 0),
+            (s_u, "Xu", slice(0, hidden_cols), 1),
+        ):
+            stride = sizes[name] // LANES
+            width = (columns.stop - columns.start) // LANES
+            first = starts[name] + (tp_place * width if width < stride else 0)
+            exit_rows(out, first, stride, columns, slot, ADAPTER_SCALING)
+
+
+def unpack(own_rows, head_cols, hidden_cols):
+    shapes = [
+        (D, LANES), (D, LANES), (LANES, D), (LANES, D), (LANES, head_cols + 2 * HD),
+        (LANES, head_cols), (LANES, hidden_cols), (LANES, hidden_cols), (LANES, hidden_cols),
+    ]
+    vmem = pl.BlockSpec(memory_space=pltpu.VMEM)
+    got = pl.pallas_call(
+        functools.partial(unpack_kernel, head_cols, hidden_cols),
+        out_shape=[jax.ShapeDtypeStruct(shape, BF16) for shape in shapes * LAYERS],
+        in_specs=[vmem],
+        out_specs=[vmem] * (len(shapes) * LAYERS),
+        scratch_shapes=[
+            pltpu.VMEM(own_rows.shape, F32), pltpu.VMEM((max(D, hidden_cols), LANES), F32),
+        ],
+        name="unpack",
+    )(own_rows)
+    maps, spares = [], []
+    for l in range(LAYERS):
+        part = got[9 * l : 9 * l + 9]
+        maps.append(dict(zip(("enter_qkv", "enter_gu", "leave_o", "leave_d"), part)))
+        spares.append(dict(zip(("qkv", "o", "g", "u", "d"), part[4:])))
+    return maps, spares
+
+
 def shards(
     hidden_in, out_grad, segments, positions, set_ids, query_w, key_w, value_w, out_w, gate_w,
     up_w, down_w, norm_gains, head_gains, adapters, first_moment, second_moment,
@@ -892,13 +1084,12 @@
     set_range = jnp.arange(set_count, dtype=jnp.int32)
 
     master_low = adapters.astype(BF16)
-    owner_sets = jnp.repeat(set_ids, tp_count)
-    selector = (owner_sets[:, None] == set_range[None, :]).astype(BF16)
+    selector = (set_ids[:, None] == set_range[None, :]).astype(BF16)
     routed = dot(selector, master_low, BF16)
     whole_rows = share % LANES == 0
-    if whole_rows:
-        routed = routed.reshape(-1, share // LANES, LANES)
-    own = lax.all_to_all(routed, ("fsdp", "tp"), split_axis=0, concat_axis=0, tiled=True)
+    tile = (share // LANES, LANES) if whole_rows else (1, share)
+    routed = routed.reshape((fsdp_count,) + tile)
+    own = lax.all_to_all(routed, "fsdp", split_axis=0, concat_axis=0, tiled=True)
 
     def local_weights(l):
         return {
@@ -928,62 +1119,15 @@
     own, late, first = lax.optimization_barrier((own, late, first))
     late_all = lax.all_gather(late, "fsdp", axis=0, tiled=True)
 
-    if whole_rows:
-        own_rows = own.reshape(-1, LANES)
-    else:
-        own_rows = own.reshape(-1).reshape(-1, LANES)
-    layer_rows = sum(n for _, n in PIECES) * RANK // LANES
-
-    def unpack(l):
-        at = l * layer_rows
-        got = {}
-        for name, n in PIECES:
-            count = n * RANK // LANES
-            rows = own_rows[at : at + count]
-            at += count
-            if name in ("Eo", "Ed"):
-                rows = lax.dynamic_slice_in_dim(rows, tp_place * (count // tp_count), count // tp_count, 0)
-            if name[0] == "X":
-                if name in ("Xq", "Xg", "Xu"):
-                    parts = n // LANES
-                    rows = rows.reshape(RANK, parts, LANES)
-                    rows = lax.dynamic_slice_in_dim(
-                        rows, tp_place * (parts // tp_count), parts // tp_count, 1
-                    )
-                got[name] = rows.reshape(RANK, -1)
-            else:
-                got[name] = expand_entry(rows)
-        return got
-
-    maps, spares = [], []
-    for l in range(LAYERS):
-        m = unpack(l)
-        m["enter_qkv"] = dot(
-            jnp.concatenate([m["Eq"], m["Ek"], m["Ev"]], axis=1),
-            jnp.concatenate([slot_pick(i) for i in range(3)], axis=0), BF16,
-        )
-        m["enter_gu"] = dot(
-            jnp.concatenate([m["Eg"], m["Eu"]], axis=1),
-            jnp.concatenate([slot_pick(i) for i in range(2)], axis=0), BF16,
-        )
-        m["leave_o"] = in_slot(ADAPTER_SCALING * m["Xo"], 0)
-        m["leave_d"] = in_slot(ADAPTER_SCALING * m["Xd"], 0)
-        spares.append({
-            "qkv": ADAPTER_SCALING * jnp.concatenate(
-                [in_slot(m["Xq"], 0), in_slot(m["Xk"], 1), in_slot(m["Xv"], 2)], axis=1
-            ),
-            "o": dot_tn(slot_pick(0), m["Eo"].T, BF16),
-            "g": ADAPTER_SCALING * in_slot(m["Xg"], 0),
-            "u": ADAPTER_SCALING * in_slot(m["Xu"], 1),
-            "d": dot_tn(slot_pick(0), m["Ed"].T, BF16),
-        })
-        maps.append(m)
+    own = pair_gather(own, 13)
+    own_rows = own.reshape(-1, LANES) if whole_rows else own.reshape(-1).reshape(-1, LANES)
+    maps, spares = unpack(own_rows, head_cols, hidden_cols)
 
     weights = [dict(), dict()]
     for (l, name), array in zip(first_names, first):
-        weights[l][name] = (array, spares[l][name].astype(BF16))
-    weights[1]["u"] = (late_all, spares[1]["u"].astype(BF16))
-    weights[1]["d"] = (late_all, spares[1]["d"].astype(BF16))
+        weights[l][name] = (array, spares[l][name])
+    weights[1]["u"] = (late_all, spares[1]["u"])
+    weights[1]["d"] = (late_all, spares[1]["d"])
     ffn_weights = [w["g"] + w["u"] + w["d"] for w in weights]
     ffn_offsets = [(0, 0, 0), (0, 0, hidden_cols)]
     cosine, sine = rope_tables(positions)

time: 863 us -> 817 us (0.947)
  Pallas kernels: 724 us -> 676 us
  waiting for transfers between devices: 37.1 us -> 68.8 us
  matrix products: 18.3 us -> 5.93 us
  other arithmetic: 15.5 us -> 6.38 us
    all_gather x1, waiting for transfers between devices: 20.5 us -> 50.1 us  [shards(): late_all = lax.all_gather(late, 'fsdp', axis=0, tiled=True)]
    pallas_call x9, Pallas kernels: 87.3 us -> 58.3 us  [exchange(): pl.pallas_call(functools.partial(exchange_kernel, body, partial is not No...]
    pallas_call x1, Pallas kernels: 309 us -> 299 us  [gather_weights(): pl.pallas_call(functools.partial(gather_kernel, plan, nz, rows, len(array...]
    pallas_call x4 -> x6, Pallas kernels: 225 us -> 218 us  [the longest x2 115 us: ffn_backward(): pl.pallas_call(functools.partial(ffn_backward_kernel, offsets, columns),...]
  transfers between devices with their start and end apart: 3 -> 3, of which waited for: 2 -> 2; matrix products, arithmetic and copies ran while one was open for 5% -> 2% of each run, Pallas kernels for 51% -> 52%
where the time goes in v1:
time: 817 us; the launch traced here: 810 us
  Pallas kernels  676 us (83%)
  waiting for transfers between devices  68.8 us (8%)
  local copies, waits for them, and re-layouts  25.6 us (3%)
  between operations  15.2 us (2%)
  starting transfers between devices  12.4 us (2%)
    pallas_call x1, Pallas kernels, gather_weights(): pl.pallas_call(functools.partial(gather_kernel, plan, nz, rows, len(array...  299 us
    pallas_call x2, Pallas kernels, ffn_backward(): pl.pallas_call(functools.partial(ffn_backward_kernel, offsets, columns),...  115 us
    pallas_call x2, Pallas kernels, ffn_forward(): pl.pallas_call(functools.partial(ffn_forward_kernel, offsets, columns), g...  86.5 us
    pallas_call x2, Pallas kernels, attention_backward(): pl.pallas_call(functools.partial(attention_backward_kernel, local_heads,...  58.8 us
    pallas_call x9, Pallas kernels, exchange(): pl.pallas_call(functools.partial(exchange_kernel, body, partial is not No...  58.3 us
    all_gather x1, waiting for transfers between devices, shards(): late_all = lax.all_gather(late, 'fsdp', axis=0, tiled=True)  50.1 us
    pallas_call x2, Pallas kernels, attention_forward(): pl.pallas_call(functools.partial(attention_forward_kernel, local_heads, s...  36.7 us
    all_to_all x1, waiting for transfers between devices, shards(): lax.all_to_all(chip_sum, 'fsdp', split_axis=0, concat_axis=0, tiled=True)  18.7 us
  transfers between devices with their start and end apart: 3, of which 2 were waited for; matrix products, arithmetic and copies ran while one was open for 2% of the time, Pallas kernels for 52%

profile of v1, /device:TPU:0, one launch (start us, length us, event | category | flops | bytes accessed | tf_op | source)
XLA Modules:
  0.0 810.3 jit_solution(10594773595457663407)
XLA Ops:
  10.3 8.3 %all-to-all-start = ((bf16[16,245,128]{2,1,0:T(8,128)(2,1)}), bf16[16,245,128]{2,1,0:T(8,128)(2,1)S(1)}, u32[]{:S(2)}, u32[]{:S(2)}) async-start(bf16[16,245,128]{2,1,0:T(8,128)(2,1)} %reshape.76), calls=%async_computation | async-start | bytes 2031616 | tf_op jit(solution)/shard_map/all_to_all | solution.py:1092
  25.6 299.1 %gather_weights.1 = (bf16[1152,1024]{1,0:T(8,128)(2,1)}, bf16[1152,512]{1,0:T(8,128)(2,1)}, bf16[1152,3456]{1,0:T(8,128)(2,1)}, bf16[1152,3456]{1,0:T(8,128)(2,1...) custom-call(bf16[72,1024]{1,0:T(8,128)(2,1)} %get-tuple-element.247., ...), custom_call_target="tpu_custom_call" | custom-call | tf_op jit(solution)/shard_map/gather_weights/pallas_call | solution.py:315
  327.5 4.8 enter.1.normed.refs_5_
  337.6 4.4 pair_gather.1
  344.8 11.4 %unpack.1 = (bf16[1152,128]{1,0:T(8,128)(2,1)}, bf16[1152,128]{1,0:T(8,128)(2,1)}, bf16[128,1152]{1,0:T(8,128)(2,1)}, bf16[128,1152]{1,0:T(8,128)(2,1)}, bf16[12...) custom-call(bf16[7840,128]{1,0:T(8,128)(2,1)} %reshape.77.rows), custom_call_target="tpu_custom_call" | custom-call | tf_op jit(solution)/shard_map/unpack/pallas_call | solution.py:1055
  356.2 18.3 %attention_forward.2 = (f32[1024,768]{1,0:T(8,128)}, bf16[1024,1024]{1,0:T(8,128)(2,1)}, bf16[1024,512]{1,0:T(8,128)(2,1)}, bf16[1024,128]{1,0:T(8,128)(2,1)}, b...) custom-call(bf16[1024,1152]{1,0:T(8,128)(2,1)} %enter.1.normed.refs_5_, ...), custom_call_target="tpu_custom_call" | custom-call | tf_op jit(solution)/shard_map/attention_forward/pallas_call | solution.py:571
  374.5 6.5 middle.2
  381.0 43.6 %ffn_forward.2 = (bf16[1024,3456]{1,0:T(8,128)(2,1)}, bf16[1024,3456]{1,0:T(8,128)(2,1)}, bf16[1024,3456]{1,0:T(8,128)(2,1)}, bf16[1024,128]{1,0:T(8,128)(2,1)},...) custom-call(bf16[1024,1152]{1,0:T(8,128)(2,1)} %get-tuple-element.124.z, ...), custom_call_target="tpu_custom_call" | custom-call | tf_op jit(solution)/shard_map/ffn_forward/pallas_call | solution.py:852
  424.6 6.3 next.1
  430.9 18.4 %attention_forward.3 = (f32[1024,768]{1,0:T(8,128)}, bf16[1024,1024]{1,0:T(8,128)(2,1)}, bf16[1024,512]{1,0:T(8,128)(2,1)}, bf16[1024,128]{1,0:T(8,128)(2,1)}, b...) custom-call(bf16[1024,1152]{1,0:T(8,128)(2,1)} %get-tuple-element.135.normed.refs_5_, ...), custom_call_target="tpu_custom_call" | custom-call | tf_op jit(solution)/shard_map/attention_forward/pallas_call | solution.py:571
  449.3 6.5 middle.3
  455.9 50.1 %all-gather.2.cloned.1.call-done.w_u.w_d = bf16[1152,6912]{1,0:T(8,128)(2,1)} async-done(((bf16[72,6912]{1,0:T(8,128)(2,1)}), bf16[1152,6912]{1,0:T(8,128)(2,1)}) %all-gather.2.cloned.1.call-update) | async-done | bytes 15925264 | tf_op jit(solution)/shard_map/all_gather | solution.py:1120
  506.0 42.9 %ffn_forward.3 = (bf16[1024,3456]{1,0:T(8,128)(2,1)}, bf16[1024,3456]{1,0:T(8,128)(2,1)}, bf16[1024,3456]{1,0:T(8,128)(2,1)}, bf16[1024,128]{1,0:T(8,128)(2,1)},...) custom-call(bf16[1024,1152]{1,0:T(8,128)(2,1)} %get-tuple-element.144.z, ...), custom_call_target="tpu_custom_call" | custom-call | tf_op jit(solution)/shard_map/ffn_forward/pallas_call | solution.py:852
  548.9 6.2 turn.1
  555.1 57.7 %ffn_backward.2 = (bf16[1024,1152]{1,0:T(8,128)(2,1)}, bf16[16,3456]{1,0:T(8,128)(2,1)}, bf16[16,3456]{1,0:T(8,128)(2,1)}, bf16[432,128]{1,0:T(8,128)(2,1)}, bf1...) custom-call(bf16[1024,1152]{1,0:T(8,128)(2,1)} %get-tuple-element.155.grad, bf16[1024,1152]{1,0:T(8,128)(2,1)} %get-tuple-element.144.z, ...), custom_call_target="tpu_custom_call" | custom-call | tf_op jit(solution)/shard_map/ffn_backward/pallas_call | solution.py:954
  612.8 7.3 back_middle.2
  620.1 29.5 %attention_backward.2 = (bf16[1024,1152]{1,0:T(8,128)(2,1)}, bf16[144,384]{1,0:T(8,128)(2,1)}, bf16[64,128]{1,0:T(8,128)(2,1)}, bf16[16,1024]{1,0:T(8,128)(2,1)}, bf16[16,1152]{1,0:T(8,128)(2,1)}) custom-call(bf16[1024,1152]{1,0:T(8,128)(2,1)} %get-tuple-element.163.grad_branch, bf16[1152,128]{1,0:T(8,128)(2,1)} %get-tuple-element.136.enter, ...), custom_call_target="tpu_custom_call" | custom-call | tf_op jit(solution)/shard_map/attention_backward/pallas_call | solution.py:701
  649.7 7.7 back_next.1
  657.4 57.6 %ffn_backward.3 = (bf16[1024,1152]{1,0:T(8,128)(2,1)}, bf16[16,3456]{1,0:T(8,128)(2,1)}, bf16[16,3456]{1,0:T(8,128)(2,1)}, bf16[432,128]{1,0:T(8,128)(2,1)}, bf1...) custom-call(bf16[1024,1152]{1,0:T(8,128)(2,1)} %get-tuple-element.173.grad, bf16[1024,1152]{1,0:T(8,128)(2,1)} %get-tuple-element.124.z, ...), custom_call_target="tpu_custom_call" | custom-call | tf_op jit(solution)/shard_map/ffn_backward/pallas_call | solution.py:954
  715.0 7.5 back_middle.3
  722.6 29.3 %attention_backward.3 = (bf16[1024,1152]{1,0:T(8,128)(2,1)}, bf16[144,384]{1,0:T(8,128)(2,1)}, bf16[64,128]{1,0:T(8,128)(2,1)}, bf16[16,1024]{1,0:T(8,128)(2,1)}, bf16[16,1152]{1,0:T(8,128)(2,1)}) custom-call(bf16[1024,1152]{1,0:T(8,128)(2,1)} %get-tuple-element.182.grad_branch, bf16[1152,128]{1,0:T(8,128)(2,1)} %get-tuple-element.117.enter, ...), custom_call_target="tpu_custom_call" | custom-call | tf_op jit(solution)/shard_map/attention_backward/pallas_call | solution.py:701
  761.8 5.5 pair_sum.1
  771.4 5.3 back_last.1
  776.7 18.7 %all-to-all-done.1 = bf16[16,245,128]{2,1,0:T(8,128)(2,1)S(1)} async-done(((bf16[16,245,128]{2,1,0:T(8,128)(2,1)}), bf16[16,245,128]{2,1,0:T(8,128)(2,1)S(1)}, u32[]{:S(2)}, u32[]{:S(2)}) %all-to-all-start.1) | async-done | bytes 1003552 | tf_op jit(solution)/shard_map/all_to_all | solution.py:1224
  (150 shorter events, 42.0 us)
Async XLA Ops:
  8.9 9.9 %copy-start.5 = (bf16[2,3456,72]{1,2,0:T(8,128)(2,1)S(1)}, bf16[2,3456,72]{1,2,0:T(8,128)(2,1)}, u32[]{:S(2)}) copy-start(bf16[2,3456,72]{1,2,0:T(8,128)(2,1)} %param.28) | copy-start | bytes 2985988
  10.3 315.4 %all-to-all-start = ((bf16[16,245,128]{2,1,0:T(8,128)(2,1)}), bf16[16,245,128]{2,1,0:T(8,128)(2,1)S(1)}, u32[]{:S(2)}, u32[]{:S(2)}) async-start(bf16[16,245,128]{2,1,0:T(8,128)(2,1)} %reshape.76), calls=%async_computation | async-start | bytes 2031616 | tf_op jit(solution)/shard_map/all_to_all | solution.py:1092
  18.7 5.8 copy-start.6
  18.7 487.3 %all-gather.2.cloned.1.call-start = ((), (), s32[]{:S(2)}) async-start(), calls=%async_computation.2 | async-start | bytes 16920576 | tf_op jit(solution)/shard_map/all_gather | solution.py:1120
  18.7 5.7 copy-start.7
  325.8 6.6 copy-start.1
  722.5 34.2 %copy-start.13 = (bf16[16,3456]{1,0:T(8,128)(2,1)S(1)}, bf16[16,3456]{1,0:T(8,128)(2,1)}, u32[]{:S(2)}) copy-start(bf16[16,3456]{1,0:T(8,128)(2,1)} %get-tuple-element.196) | copy-start | bytes 331780
  722.6 35.4 %copy-start.17 = (bf16[144,256]{1,0:T(8,128)(2,1)S(1)}, bf16[144,256]{1,0:T(8,128)(2,1)}, u32[]{:S(2)}) copy-start(bf16[144,256]{1,0:T(8,128)(2,1)} %get-tuple-element.195) | copy-start | bytes 221188
  751.9 6.2 copy-start.12
  751.9 6.5 copy-start.20
  751.9 6.6 copy-start.21
  752.8 5.9 copy-start.11
  756.7 2.0 copy-start.14
  756.8 2.1 copy-start.19
  757.1 1.9 copy-start.10
  758.0 1.4 copy-start.23
  758.0 1.4 copy-start.16
  758.8 1.3 copy-start.8
  767.3 28.1 %all-to-all-start.1 = ((bf16[16,245,128]{2,1,0:T(8,128)(2,1)}), bf16[16,245,128]{2,1,0:T(8,128)(2,1)S(1)}, u32[]{:S(2)}, u32[]{:S(2)}) async-start(bf16[16,245,128]{2,1,0:T(8,128)(2,1)} %pair_sum.1), calls=%async_computation.1 | async-start | bytes 2031616 | tf_op jit(solution)/shard_map/all_to_all | solution.py:1224
  771.4 24.1 %copy-start.2 = (f32[8,31360]{1,0:T(8,128)S(1)}, f32[8,31360]{1,0:T(8,128)}, u32[]{:S(2)}) copy-start(f32[8,31360]{1,0:T(8,128)} %param.31) | copy-start | bytes 3010564
  771.4 24.1 %copy-start.4 = (f32[8,31360]{1,0:T(8,128)S(1)}, f32[8,31360]{1,0:T(8,128)}, u32[]{:S(2)}) copy-start(f32[8,31360]{1,0:T(8,128)} %param.32) | copy-start | bytes 3010564
  771.4 24.1 %copy-start.25 = (s32[16]{0:T(128)S(1)}, s32[16]{0:T(128)}, u32[]{:S(2)}) copy-start(s32[16]{0:T(128)} %param.21) | copy-start | bytes 196
  795.5 4.2 copy-start.3
  799.7 2.1 copy-start
  (6 other events, 6.9 us)
Sparse Core Ops, SparseCore 0:
  325.9 180.0 all-gather.1

commit v2 on v1

--- a/solution.py
+++ b/solution.py
@@ -31,7 +31,7 @@
 F32 = jnp.float32
 BF16 = jnp.bfloat16
 MESH = pl.DeviceIdType.MESH
-EXCHANGE_CHUNKS = 8
+EXCHANGE_CHUNKS = 4
 
 PIECES = (
     ("Eq", D), ("Xq", HEADS * HD), ("Ek", D), ("Xk", HD), ("Ev", D), ("Xv", HD),
@@ -369,7 +369,9 @@
     )(partial)
 
 
-def pair_gather_kernel(count, mine, both, send_sem, recv_sem, local_sem):
+def pair_gather_kernel(count, n_arrays, mine, *refs):
+    arrays, both, halves = refs[:n_arrays], refs[n_arrays], refs[n_arrays + 1 : 2 * n_arrays + 1]
+    send_sem, recv_sem, local_sem, send_half, recv_half = refs[2 * n_arrays + 1 :]
     me = lax.axis_index("tp")
     other = 1 - me
     barrier = pltpu.get_barrier_semaphore()
@@ -385,23 +387,37 @@
             )
         )
         copies.append(pltpu.make_async_copy(mine.at[i], place, local_sem.at[i]))
+    for i in range(n_arrays):
+        columns = halves[i].shape[1]
+        first = arrays[i].shape[1] - columns
+        copies.append(
+            pltpu.make_async_remote_copy(
+                src_ref=arrays[i].at[:, pl.ds(first, columns)], dst_ref=halves[i],
+                send_sem=send_half.at[i], recv_sem=recv_half.at[i],
+                device_id={"tp": other}, device_id_type=MESH,
+            )
+        )
     for copy in copies:
         copy.start()
     for copy in copies:
         copy.wait()
 
 
-def pair_gather(mine, collective_id):
+def pair_gather(mine, arrays, columns, collective_id):
     count = mine.shape[0]
-    return pl.pallas_call(
-        functools.partial(pair_gather_kernel, count),
-        out_shape=jax.ShapeDtypeStruct((2 * count,) + mine.shape[1:], mine.dtype),
-        in_specs=[pl.BlockSpec(memory_space=pltpu.VMEM)],
-        out_specs=pl.BlockSpec(memory_space=pl.ANY),
-        scratch_shapes=[pltpu.SemaphoreType.DMA((count,))] * 3,
+    hbm = pl.BlockSpec(memory_space=pl.ANY)
+    got = pl.pallas_call(
+        functools.partial(pair_gather_kernel, count, len(arrays)),
+        out_shape=[jax.ShapeDtypeStruct((2 * count,) + mine.shape[1:], mine.dtype)]
+        + [jax.ShapeDtypeStruct((a.shape[0], columns), a.dtype) for a in arrays],
+        in_specs=[pl.BlockSpec(memory_space=pltpu.VMEM)] + [hbm] * len(arrays),
+        out_specs=[hbm] * (1 + len(arrays)),
+        scratch_shapes=[pltpu.SemaphoreType.DMA((count,))] * 3
+        + [pltpu.SemaphoreType.DMA((len(arrays),))] * 2,
         compiler_params=pltpu.CompilerParams(collective_id=collective_id, has_side_effects=True),
         name="pair_gather",
-    )(mine)
+    )(mine, *arrays)
+    return got[0], got[1:]
 
 
 def body_enter(total, rows, gains):
@@ -495,16 +511,35 @@
     return out
 
 
-def with_slots(weight):
-    return pltpu.VMEM((weight.shape[0] + LANES, weight.shape[1]), BF16)
+def qkv_copies(own, slots, partner, target, sems):
+    me = lax.axis_index("tp")
+    rows, half = own.shape[0], partner.shape[1] // 2
+    heads = own.shape[1] - 2 * half
+    top = pl.ds(0, rows)
+
+    def columns(part, core):
+        return pl.ds(pl.multiple_of(heads + part * 2 * half + core * half, half), half)
+
+    pairs = [
+        (own.at[:, pl.ds(0, heads)], target.at[top, pl.ds(0, heads)]),
+        (slots, target.at[pl.ds(rows, slots.shape[0])]),
+    ]
+    for part in range(2):
+        pairs.append((own.at[:, pl.ds(heads + part * half, half)], target.at[top, columns(part, me)]))
+        pairs.append((partner.at[:, pl.ds(part * half, half)], target.at[top, columns(part, 1 - me)]))
+    return [pltpu.make_async_copy(*pair, sems.at[i]) for i, pair in enumerate(pairs)]
+
+
+def with_slots(parts):
+    return pltpu.VMEM((parts[0].shape[0] + LANES, parts[1].shape[1]), BF16)
 
 
 def attention_forward_kernel(
     local_heads, scale, normed, enter, leave, gains, cosine, sine, segment_column, segment_row,
-    w_qkv, w_o, s_qkv, s_o, raw, qkv, attn, mid_qkv, mid_o, stats, share, w_qkv_here, w_o_here, sems,
+    w_qkv, w_o, s_qkv, s_o, w_kv, raw, qkv, attn, mid_qkv, mid_o, stats, share, w_qkv_here, w_o_here, sems,
 ):
     copies = [
-        weight_copies((w_qkv, s_qkv), w_qkv_here, sems.at[0]),
+        qkv_copies(w_qkv, s_qkv, w_kv, w_qkv_here, sems.at[0]),
         weight_copies((w_o, s_o), w_o_here, sems.at[1]),
     ]
     for c in copies[0] + copies[1]:
@@ -560,7 +595,7 @@
 def attention_forward(normed, enter, leave, gains, cosine, sine, segments, qkv_parts, o_parts, scale):
     w_qkv, w_o = qkv_parts[0], o_parts[0]
     length, width = normed.shape
-    columns = w_qkv.shape[1]
+    columns = qkv_parts[1].shape[1]
     local_heads = columns // HD - 2
     shapes = [
         ((length, columns - HD), F32), ((length, columns), BF16), ((length, local_heads * HD), BF16),
@@ -571,14 +606,14 @@
     return pl.pallas_call(
         functools.partial(attention_forward_kernel, local_heads, scale),
         out_shape=[jax.ShapeDtypeStruct(*shape) for shape in shapes],
-        in_specs=[vmem] * 8 + [pl.BlockSpec(memory_space=pl.ANY)] * 4,
+        in_specs=[vmem] * 8 + [pl.BlockSpec(memory_space=pl.ANY)] * 5,
         out_specs=[vmem] * len(shapes),
         scratch_shapes=[
-            with_slots(w_qkv), with_slots(w_o), pltpu.SemaphoreType.DMA((2, 2)),
+            with_slots(qkv_parts), with_slots(o_parts), pltpu.SemaphoreType.DMA((2, 6)),
         ],
         name="attention_forward",
     )(normed, enter, leave, gains, cosine, sine, segments[:, None], segments[None, :], w_qkv, w_o,
-        qkv_parts[1], o_parts[1])
+        qkv_parts[1], o_parts[1], qkv_parts[2])
 
 
 def fold_rows(wide):
@@ -592,14 +627,14 @@
     local_heads, scale, grad_branch, enter, leave, gains, segment_column, segment_row, spread, *refs
 ):
     distant, refs = refs[:9], refs[9:]
-    w_qkv, w_o, s_qkv, s_o, share, entry_qkv, entry_o, exit_qkv, exit_o = refs[:9]
-    w_qkv_here, w_o_here, grad_attn, grad_raw, grad_k, grad_v, spread_qkv, spread_o, sems = refs[9:18]
-    near, near_sems = refs[18:27], refs[27]
+    w_qkv, w_o, s_qkv, s_o, w_kv, share, entry_qkv, entry_o, exit_qkv, exit_o = refs[:10]
+    w_qkv_here, w_o_here, grad_attn, grad_raw, grad_k, grad_v, spread_qkv, spread_o, sems = refs[10:19]
+    near, near_sems = refs[19:28], refs[28]
     loads = [pltpu.make_async_copy(*pair, near_sems.at[i]) for i, pair in enumerate(zip(distant, near))]
     qkv, stats, raw, cosine, sine, normed, attn, mid_qkv, mid_o = near
     copies = [
         weight_copies((w_o, s_o), w_o_here, sems.at[0]),
-        weight_copies((w_qkv, s_qkv), w_qkv_here, sems.at[1]),
+        qkv_copies(w_qkv, s_qkv, w_kv, w_qkv_here, sems.at[1]),
     ]
     for c in copies[0] + loads[:5] + copies[1] + loads[5:]:
         c.start()
@@ -611,7 +646,7 @@
     for c in copies[0]:
         c.wait()
 
-    @pl.loop(0, blocks)
+    @pl.loop(0, blocks, unroll=2)
     def _(i):
         rows = rows_at(i)
         g = grad_branch[rows, :]
@@ -622,7 +657,7 @@
     for c in loads[:5]:
         c.wait()
 
-    @pl.loop(0, blocks)
+    @pl.loop(0, blocks, unroll=2)
     def _(i):
         rows = rows_at(i)
         first = key_start(i)
@@ -649,7 +684,7 @@
     for c in copies[1]:
         c.wait()
 
-    @pl.loop(0, blocks)
+    @pl.loop(0, blocks, unroll=2)
     def _(i):
         rows = rows_at(i)
         grad_raw[rows, key_col:value_col] = head_backward(
@@ -686,7 +721,7 @@
 ):
     w_qkv, w_o = qkv_parts[0], o_parts[0]
     length, width = grad_branch.shape
-    columns = w_qkv.shape[1]
+    columns = qkv_parts[1].shape[1]
     local_heads = columns // HD - 2
     spread = jnp.concatenate([slot_spread(i) for i in range(3)], axis=1)
     distant = [
@@ -701,21 +736,21 @@
     return pl.pallas_call(
         functools.partial(attention_backward_kernel, local_heads, scale),
         out_shape=[jax.ShapeDtypeStruct(shape, BF16) for shape in shapes],
-        in_specs=[vmem] * 7 + [pl.BlockSpec(memory_space=pl.ANY)] * 13,
+        in_specs=[vmem] * 7 + [pl.BlockSpec(memory_space=pl.ANY)] * 14,
         out_specs=[vmem] * len(shapes),
         scratch_shapes=[
-            with_slots(w_qkv), with_slots(w_o),
+            with_slots(qkv_parts), with_slots(o_parts),
             pltpu.VMEM((length, local_heads * HD), BF16), pltpu.VMEM((length, columns), BF16),
             pltpu.VMEM((length, HD), F32), pltpu.VMEM((length, HD), F32),
             pltpu.VMEM((length, 3 * LANES), BF16), pltpu.VMEM((length, LANES), BF16),
-            pltpu.SemaphoreType.DMA((2, 2)),
+            pltpu.SemaphoreType.DMA((2, 6)),
         ]
         + [pltpu.VMEM(a.shape, a.dtype) for a in distant]
         + [pltpu.SemaphoreType.DMA((len(distant),))],
         name="attention_backward",
     )(
         grad_branch, enter, leave, gains, segments[:, None], segments[None, :], spread, *distant,
-        w_qkv, w_o, qkv_parts[1], o_parts[1],
+        w_qkv, w_o, qkv_parts[1], o_parts[1], qkv_parts[2],
     )
 
 
@@ -866,6 +901,129 @@
         compiler_params=pltpu.CompilerParams(vmem_limit_bytes=VMEM_LIMIT),
         name="ffn_forward",
     )(z, enter, leave, *weights)
+
+
+def ffn_gate_kernel(offsets, columns, z, enter, w_g, s_g, gelu, rate, mid_gu, buffers, joined, sems):
+    j = pl.program_id(0)
+    slot = j % 2
+    width = z.shape[1]
+    blocks = z.shape[0] // ROW_BLOCK
+    ffn_start((w_g, s_g), offsets, buffers, sems, (0,), columns)
+
+    @pl.when(j == 0)
+    def _():
+        mid = dot(z[...], enter[...], BF16)
+        mid_gu[...] = mid
+        joined[:, :width] = z[...]
+        joined[:, width:] = mid
+
+    def step(count):
+        for c in ffn_fetch((w_g, s_g), offsets, buffers, sems, 0, j, slot, count):
+            c.wait()
+
+        @pl.loop(0, blocks)
+        def _(i):
+            rows = rows_at(i)
+            value, change = gelu_parts(dot(joined[rows, :], buffers[0, slot, :, :count]))
+            gelu[rows, :count] = value.astype(BF16)
+            rate[rows, :count] = change.astype(BF16)
+
+    by_width(columns, step)
+
+
+def ffn_gate(z, enter, weights):
+    length, width = z.shape
+    columns = weights[1].shape[1]
+
+    def fixed(shape):
+        return pl.BlockSpec(shape, lambda j: (0, 0), pipeline_mode=pl.Buffered(1))
+
+    wide = pl.BlockSpec((length, FFN_BLOCK), lambda j: (0, j))
+    return pl.pallas_call(
+        functools.partial(ffn_gate_kernel, (0,), columns),
+        grid=(pl.cdiv(columns, FFN_BLOCK),),
+        out_shape=[jax.ShapeDtypeStruct((length, columns), BF16)] * 2
+        + [jax.ShapeDtypeStruct((length, LANES), BF16)],
+        in_specs=[fixed(z.shape), fixed(enter.shape)] + [pl.BlockSpec(memory_space=pl.ANY)] * 2,
+        out_specs=[wide, wide, fixed((length, LANES))],
+        scratch_shapes=[
+            pltpu.VMEM((1, 2, width + LANES, FFN_BLOCK), BF16),
+            pltpu.VMEM((length, width + LANES), BF16),
+            pltpu.SemaphoreType.DMA((1, 2, 2)),
+        ],
+        compiler_params=pltpu.CompilerParams(vmem_limit_bytes=VMEM_LIMIT),
+        name="ffn_gate",
+    )(z, enter, *weights)
+
+
+def ffn_rest_kernel(
+    offsets, columns, z, mid_gu, leave, gelu, rate, w_u, s_u, w_d, s_d,
+    slope, hidden, mid_d, share, buffers, joined, total, sems,
+):
+    j = pl.program_id(0)
+    slot = j % 2
+    width = z.shape[1]
+    blocks = z.shape[0] // ROW_BLOCK
+    weights = (w_u, s_u, w_d, s_d)
+    ffn_start(weights, offsets, buffers, sems, (0, 1), columns)
+
+    @pl.when(j == 0)
+    def _():
+        joined[:, :width] = z[...]
+        joined[:, width:] = mid_gu[...]
+
+    def step(count):
+        def wait(k):
+            for c in ffn_fetch(weights, offsets, buffers, sems, k, j, slot, count):
+                c.wait()
+
+        wait(0)
+
+        @pl.loop(0, blocks)
+        def _(i):
+            rows = rows_at(i)
+            up_pre = dot(joined[rows, :], buffers[0, slot, :, :count])
+            slope[rows, :count] = (rate[rows, :count].astype(F32) * up_pre).astype(BF16)
+            hidden[rows, :count] = (gelu[rows, :count].astype(F32) * up_pre).astype(BF16)
+
+        wait(1)
+        add_to(total, dot_nt(hidden[:, :count], buffers[1, slot, :, :count]))
+
+    by_width(columns, step)
+
+    @pl.when(j == pl.num_programs(0) - 1)
+    def _():
+        mid = total[:, width:].astype(BF16)
+        mid_d[...] = mid
+        share[...] = (total[:, :width] + dot(mid, leave[...])).astype(BF16)
+
+
+def ffn_rest(z, mid_gu, leave, gelu, rate, weights, offsets):
+    length, width = z.shape
+    columns = weights[1].shape[1]
+
+    def fixed(shape):
+        return pl.BlockSpec(shape, lambda j: (0, 0), pipeline_mode=pl.Buffered(1))
+
+    wide = pl.BlockSpec((length, FFN_BLOCK), lambda j: (0, j))
+    small = (length, LANES)
+    return pl.pallas_call(
+        functools.partial(ffn_rest_kernel, offsets, columns),
+        grid=(pl.cdiv(columns, FFN_BLOCK),),
+        out_shape=[jax.ShapeDtypeStruct((length, columns), BF16)] * 2
+        + [jax.ShapeDtypeStruct(small, BF16), jax.ShapeDtypeStruct((length, width), BF16)],
+        in_specs=[fixed(z.shape), fixed(small), fixed(leave.shape), wide, wide]
+        + [pl.BlockSpec(memory_space=pl.ANY)] * 4,
+        out_specs=[wide, wide, fixed(small), fixed((length, width))],
+        scratch_shapes=[
+            pltpu.VMEM((2, 2, width + LANES, FFN_BLOCK), BF16),
+            pltpu.VMEM((length, width + LANES), BF16),
+            pltpu.VMEM((length, width + LANES), F32),
+            pltpu.SemaphoreType.DMA((2, 2, 2)),
+        ],
+        compiler_params=pltpu.CompilerParams(vmem_limit_bytes=VMEM_LIMIT),
+        name="ffn_rest",
+    )(z, mid_gu, leave, gelu, rate, *weights)
 
 
 def ffn_backward_kernel(
@@ -1083,17 +1241,16 @@
     scale = HD ** (-0.5)
     set_range = jnp.arange(set_count, dtype=jnp.int32)
 
-    master_low = adapters.astype(BF16)
     selector = (set_ids[:, None] == set_range[None, :]).astype(BF16)
-    routed = dot(selector, master_low, BF16)
     whole_rows = share % LANES == 0
     tile = (share // LANES, LANES) if whole_rows else (1, share)
-    routed = routed.reshape((fsdp_count,) + tile)
-    own = lax.all_to_all(routed, "fsdp", split_axis=0, concat_axis=0, tiled=True)
+
+    def core_half(w):
+        return lax.dynamic_slice_in_dim(w, tp_place * (HD // tp_count), HD // tp_count, 1)
 
     def local_weights(l):
         return {
-            "qkv": jnp.concatenate([query_w[l], key_w[l], value_w[l]], axis=1),
+            "qkv": jnp.concatenate([query_w[l], core_half(key_w[l]), core_half(value_w[l])], axis=1),
             "o": out_w[l].T,
             "g": gate_w[l],
             "u": up_w[l],
@@ -1116,16 +1273,18 @@
         first = gather_weights(arrays, plan, fsdp_count, 11)
     else:
         first = [lax.all_gather(a, "fsdp", axis=0, tiled=True) for a in arrays]
-    own, late, first = lax.optimization_barrier((own, late, first))
+    master_low, late, first = lax.optimization_barrier((adapters, late, first))
     late_all = lax.all_gather(late, "fsdp", axis=0, tiled=True)
-
-    own = pair_gather(own, 13)
+    routed = dot(selector, master_low.astype(BF16), BF16).reshape((fsdp_count,) + tile)
+    own = lax.all_to_all(routed, "fsdp", split_axis=0, concat_axis=0, tiled=True)
+
+    own, key_values = pair_gather(own, [first[first_names.index((l, "qkv"))] for l in range(LAYERS)], HD, 13)
     own_rows = own.reshape(-1, LANES) if whole_rows else own.reshape(-1).reshape(-1, LANES)
     maps, spares = unpack(own_rows, head_cols, hidden_cols)
 
     weights = [dict(), dict()]
     for (l, name), array in zip(first_names, first):
-        weights[l][name] = (array, spares[l][name])
+        weights[l][name] = (array, spares[l][name]) + ((key_values[l],) if name == "qkv" else ())
     weights[1]["u"] = (late_all, spares[1]["u"])
     weights[1]["d"] = (late_all, spares[1]["d"])
     ffn_weights = [w["g"] + w["u"] + w["d"] for w in weights]
@@ -1154,9 +1313,16 @@
             body_middle, 2 if l == 0 else 3, "middle", share_o, [x], [gain(l, 1), gain(l, 2)],
             [F32, F32], True,
         )
-        r["gelu"], r["slope"], r["hidden"], r["mid_gu"], r["mid_d"], share_f = ffn_forward(
-            r["normed_two"], m["enter_gu"], m["leave_d"], ffn_weights[l], ffn_offsets[l]
-        )
+        if l == 0:
+            r["gelu"], r["slope"], r["hidden"], r["mid_gu"], r["mid_d"], share_f = ffn_forward(
+                r["normed_two"], m["enter_gu"], m["leave_d"], ffn_weights[l], ffn_offsets[l]
+            )
+        else:
+            r["gelu"], rate, r["mid_gu"] = ffn_gate(r["normed_two"], m["enter_gu"], w["g"])
+            r["slope"], r["hidden"], r["mid_d"], share_f = ffn_rest(
+                r["normed_two"], r["mid_gu"], m["leave_d"], r["gelu"], rate, w["u"] + w["d"],
+                ffn_offsets[l][1:],
+            )
         if l + 1 < LAYERS:
             r["ffn_branch"], x, normed = exchange(
                 body_next, 4, "next", share_f, [r["middle"]], [gain(l, 3), gain(l + 1, 0)],

time: 817 us -> 796 us (0.974)
  waiting for transfers between devices: 68.8 us -> 55.9 us
    pallas_call x1 -> x3, Pallas kernels: 4.39 us -> 64.2 us  [the longest x1 34.2 us: ffn_rest(): pl.pallas_call(functools.partial(ffn_rest_kernel, offsets, columns), grid...]
    pallas_call x2 -> x1, Pallas kernels: 86.5 us -> 43.2 us  [ffn_forward(): pl.pallas_call(functools.partial(ffn_forward_kernel, offsets, columns), g...]
    all_gather x1, waiting for transfers between devices: 50.1 us -> 12.2 us  [shards(): late_all = lax.all_gather(late, 'fsdp', axis=0, tiled=True)]
    all_to_all x1, waiting for transfers between devices: 0.01 us -> 25.1 us  [shards(): lax.all_to_all(routed, 'fsdp', split_axis=0, concat_axis=0, tiled=True)]
    pallas_call x1, Pallas kernels: 299 us -> 287 us  [gather_weights(): pl.pallas_call(functools.partial(gather_kernel, plan, nz, rows, len(array...]
  transfers between devices with their start and end apart: 3 -> 3, of which waited for: 2 -> 3; matrix products, arithmetic and copies ran while one was open for 2% -> 1% of each run, Pallas kernels for 52% -> 19%
where the time goes in v2:
time: 796 us; the launch traced here: 790 us
  Pallas kernels  673 us (85%)
  waiting for transfers between devices  55.9 us (7%)
  local copies, waits for them, and re-layouts  26.9 us (3%)
  between operations  15.2 us (2%)
    pallas_call x1, Pallas kernels, gather_weights(): pl.pallas_call(functools.partial(gather_kernel, plan, nz, rows, len(array...  287 us
    pallas_call x2, Pallas kernels, ffn_backward(): pl.pallas_call(functools.partial(ffn_backward_kernel, offsets, columns),...  115 us
    pallas_call x9, Pallas kernels, exchange(): pl.pallas_call(functools.partial(exchange_kernel, body, partial is not No...  57.5 us
    pallas_call x2, Pallas kernels, attention_backward(): pl.pallas_call(functools.partial(attention_backward_kernel, local_heads,...  52 us
    pallas_call x1, Pallas kernels, ffn_forward(): pl.pallas_call(functools.partial(ffn_forward_kernel, offsets, columns), g...  43.2 us
    pallas_call x2, Pallas kernels, attention_forward(): pl.pallas_call(functools.partial(attention_forward_kernel, local_heads, s...  36.9 us
    pallas_call x1, Pallas kernels, ffn_rest(): pl.pallas_call(functools.partial(ffn_rest_kernel, offsets, columns), grid...  34.2 us
    all_to_all x1, waiting for transfers between devices, shards(): lax.all_to_all(routed, 'fsdp', split_axis=0, concat_axis=0, tiled=True)  25.1 us
  transfers between devices with their start and end apart: 3, of which 3 were waited for; matrix products, arithmetic and copies ran while one was open for 1% of the time, Pallas kernels for 19%

profile of v2, /device:TPU:0, one launch (start us, length us, event | category | flops | bytes accessed | tf_op | source)
XLA Modules:
  0.0 789.9 jit_solution(1616820151761873864)
XLA Ops:
  16.1 286.7 %gather_weights.1 = (bf16[1152,768]{1,0:T(8,128)(2,1)}, bf16[1152,512]{1,0:T(8,128)(2,1)}, bf16[1152,3456]{1,0:T(8,128)(2,1)}, bf16[1152,3456]{1,0:T(8,128)(2,1)...) custom-call(bf16[72,768]{1,0:T(8,128)(2,1)} %pad_maximum_fusion.1.re, ...), custom_call_target="tpu_custom_call" | custom-call | tf_op jit(solution)/shard_map/gather_weights/pallas_call | solution.py:315
  320.2 25.1 %all-to-all-done.mine = bf16[16,245,128]{2,1,0:T(8,128)(2,1)S(1)} async-done(((bf16[16,245,128]{2,1,0:T(8,128)(2,1)}), bf16[16,245,128]{2,1,0:T(8,128)(2,1)S(1)}, u32[]{:S(2)}, u32[]{:S(2)}) %all-to-all-start) | async-done | bytes 1003552 | tf_op jit(solution)/shard_map/all_to_all | solution.py:1279
  346.3 6.1 pair_gather.1
  355.2 11.4 %unpack.1 = (bf16[1152,128]{1,0:T(8,128)(2,1)}, bf16[1152,128]{1,0:T(8,128)(2,1)}, bf16[128,1152]{1,0:T(8,128)(2,1)}, bf16[128,1152]{1,0:T(8,128)(2,1)}, bf16[12...) custom-call(bf16[7840,128]{1,0:T(8,128)(2,1)} %reshape.81.rows), custom_call_target="tpu_custom_call" | custom-call | tf_op jit(solution)/shard_map/unpack/pallas_call | solution.py:1213
  366.6 18.2 %attention_forward.2 = (f32[1024,768]{1,0:T(8,128)}, bf16[1024,1024]{1,0:T(8,128)(2,1)}, bf16[1024,512]{1,0:T(8,128)(2,1)}, bf16[1024,128]{1,0:T(8,128)(2,1)}, b...) custom-call(bf16[1024,1152]{1,0:T(8,128)(2,1)} %enter.1.normed.refs_5_, ...), custom_call_target="tpu_custom_call" | custom-call | tf_op jit(solution)/shard_map/attention_forward/pallas_call | solution.py:606
  384.8 6.2 middle.2
  391.0 43.2 %ffn_forward.1 = (bf16[1024,3456]{1,0:T(8,128)(2,1)}, bf16[1024,3456]{1,0:T(8,128)(2,1)}, bf16[1024,3456]{1,0:T(8,128)(2,1)}, bf16[1024,128]{1,0:T(8,128)(2,1)},...) custom-call(bf16[1024,1152]{1,0:T(8,128)(2,1)} %get-tuple-element.131.z, ...), custom_call_target="tpu_custom_call" | custom-call | tf_op jit(solution)/shard_map/ffn_forward/pallas_call | solution.py:887
  434.2 6.4 next.1
  440.6 18.7 %attention_forward.3 = (f32[1024,768]{1,0:T(8,128)}, bf16[1024,1024]{1,0:T(8,128)(2,1)}, bf16[1024,512]{1,0:T(8,128)(2,1)}, bf16[1024,128]{1,0:T(8,128)(2,1)}, b...) custom-call(bf16[1024,1152]{1,0:T(8,128)(2,1)} %get-tuple-element.142.normed.refs_5_, ...), custom_call_target="tpu_custom_call" | custom-call | tf_op jit(solution)/shard_map/attention_forward/pallas_call | solution.py:606
  459.3 6.2 middle.3
  465.5 23.9 %ffn_gate.1 = (bf16[1024,3456]{1,0:T(8,128)(2,1)}, bf16[1024,3456]{1,0:T(8,128)(2,1)}, bf16[1024,128]{1,0:T(8,128)(2,1)}) custom-call(bf16[1024,1152]{1,0:T(8,128)(2,1)} %get-tuple-element.151.z, bf16[1152,128]{1,0:T(8,128)(2,1)} %get-tuple-element.152.enter, bf16[1152,3456]{1,0:T(8,128)(2,1)} %get-tuple-element.153.w_g, ...), custom_call_target="tpu_custom_call" | custom-call | tf_op jit(solution)/shard_map/ffn_gate/pallas_call | solution.py:942
  489.4 12.2 %all-gather.2.cloned.1.call-done.w_u.w_d = bf16[1152,6912]{1,0:T(8,128)(2,1)} async-done(((bf16[72,6912]{1,0:T(8,128)(2,1)}), bf16[1152,6912]{1,0:T(8,128)(2,1)}) %all-gather.2.cloned.1.call-update) | async-done | bytes 15925264 | tf_op jit(solution)/shard_map/all_gather | solution.py:1277
  501.6 34.2 %ffn_rest.1 = (bf16[1024,3456]{1,0:T(8,128)(2,1)}, bf16[1024,3456]{1,0:T(8,128)(2,1)}, bf16[1024,128]{1,0:T(8,128)(2,1)}, bf16[1024,1152]{1,0:T(8,128)(2,1)}) custom-call(bf16[1024,1152]{1,0:T(8,128)(2,1)} %get-tuple-element.151.z, bf16[1024,128]{1,0:T(8,128)(2,1)} %get-tuple-element.155.mid_gu, bf16[128,1152]{1,0:T(8,128)(2,1)} %get-tuple-element.156.leave, ...), custom_call_target="tpu_custom_call" | custom-call | tf_op jit(solution)/shard_map/ffn_rest/pallas_call | solution.py:1010
  535.8 6.2 turn.1
  542.0 57.7 %ffn_backward.2 = (bf16[1024,1152]{1,0:T(8,128)(2,1)}, bf16[16,3456]{1,0:T(8,128)(2,1)}, bf16[16,3456]{1,0:T(8,128)(2,1)}, bf16[432,128]{1,0:T(8,128)(2,1)}, bf1...) custom-call(bf16[1024,1152]{1,0:T(8,128)(2,1)} %get-tuple-element.165.grad, bf16[1024,1152]{1,0:T(8,128)(2,1)} %get-tuple-element.151.z, ...), custom_call_target="tpu_custom_call" | custom-call | tf_op jit(solution)/shard_map/ffn_backward/pallas_call | solution.py:1112
  599.7 7.4 back_middle.2
  607.1 25.9 %attention_backward.2 = (bf16[1024,1152]{1,0:T(8,128)(2,1)}, bf16[144,384]{1,0:T(8,128)(2,1)}, bf16[64,128]{1,0:T(8,128)(2,1)}, bf16[16,1024]{1,0:T(8,128)(2,1)}, bf16[16,1152]{1,0:T(8,128)(2,1)}) custom-call(bf16[1024,1152]{1,0:T(8,128)(2,1)} %get-tuple-element.171.grad_branch, bf16[1152,128]{1,0:T(8,128)(2,1)} %get-tuple-element.143.enter, ...), custom_call_target="tpu_custom_call" | custom-call | tf_op jit(solution)/shard_map/attention_backward/pallas_call | solution.py:736
  632.9 7.4 back_next.1
  640.3 57.7 %ffn_backward.3 = (bf16[1024,1152]{1,0:T(8,128)(2,1)}, bf16[16,3456]{1,0:T(8,128)(2,1)}, bf16[16,3456]{1,0:T(8,128)(2,1)}, bf16[432,128]{1,0:T(8,128)(2,1)}, bf1...) custom-call(bf16[1024,1152]{1,0:T(8,128)(2,1)} %get-tuple-element.181.grad, bf16[1024,1152]{1,0:T(8,128)(2,1)} %get-tuple-element.131.z, ...), custom_call_target="tpu_custom_call" | custom-call | tf_op jit(solution)/shard_map/ffn_backward/pallas_call | solution.py:1112
  698.0 7.6 back_middle.3
  705.7 26.1 %attention_backward.3 = (bf16[1024,1152]{1,0:T(8,128)(2,1)}, bf16[144,384]{1,0:T(8,128)(2,1)}, bf16[64,128]{1,0:T(8,128)(2,1)}, bf16[16,1024]{1,0:T(8,128)(2,1)}, bf16[16,1152]{1,0:T(8,128)(2,1)}) custom-call(bf16[1024,1152]{1,0:T(8,128)(2,1)} %get-tuple-element.190.grad_branch, bf16[1152,128]{1,0:T(8,128)(2,1)} %get-tuple-element.124.enter, ...), custom_call_target="tpu_custom_call" | custom-call | tf_op jit(solution)/shard_map/attention_backward/pallas_call | solution.py:736
  741.7 5.5 pair_sum.1
  751.1 5.4 back_last.1
  756.5 18.6 %all-to-all-done.1 = bf16[16,245,128]{2,1,0:T(8,128)(2,1)S(1)} async-done(((bf16[16,245,128]{2,1,0:T(8,128)(2,1)}), bf16[16,245,128]{2,1,0:T(8,128)(2,1)S(1)}, u32[]{:S(2)}, u32[]{:S(2)}) %all-to-all-start.1) | async-done | bytes 1003552 | tf_op jit(solution)/shard_map/all_to_all | solution.py:1390
  (156 shorter events, 50.8 us)
Async XLA Ops:
  7.2 4.8 copy-start.8
  7.2 5.5 copy-start.6
  7.2 5.5 copy-start.7
  7.2 494.4 %all-gather.2.cloned.1.call-start = ((), (), s32[]{:S(2)}) async-start(), calls=%async_computation.2 | async-start | bytes 16920576 | tf_op jit(solution)/shard_map/all_gather | solution.py:1277
  14.8 288.1 %copy-start.2 = (f32[8,31360]{1,0:T(8,128)S(1)}, f32[8,31360]{1,0:T(8,128)}, u32[]{:S(2)}) copy-start(f32[8,31360]{1,0:T(8,128)} %param.31) | copy-start | bytes 3010564
  14.8 288.1 %copy-start.26 = (s32[16]{0:T(128)S(1)}, s32[16]{0:T(128)}, u32[]{:S(2)}) copy-start(s32[16]{0:T(128)} %param.21) | copy-start | bytes 196
  303.4 5.4 copy-start.23
  303.4 5.4 copy-start.25
  303.4 5.4 copy-start.16
  303.4 6.4 copy-start.27
  304.9 40.5 %all-to-all-start = ((bf16[16,245,128]{2,1,0:T(8,128)(2,1)}), bf16[16,245,128]{2,1,0:T(8,128)(2,1)S(1)}, u32[]{:S(2)}, u32[]{:S(2)}) async-start(bf16[16,245,128]{2,1,0:T(8,128)(2,1)} %reshape.80), calls=%async_computation | async-start | bytes 2031616 | tf_op jit(solution)/shard_map/all_to_all | solution.py:1279
  705.6 31.0 %copy-start.14 = (bf16[16,3456]{1,0:T(8,128)(2,1)S(1)}, bf16[16,3456]{1,0:T(8,128)(2,1)}, u32[]{:S(2)}) copy-start(bf16[16,3456]{1,0:T(8,128)(2,1)} %get-tuple-element.204) | copy-start | bytes 331780
  705.7 32.2 %copy-start.18 = (bf16[144,256]{1,0:T(8,128)(2,1)S(1)}, bf16[144,256]{1,0:T(8,128)(2,1)}, u32[]{:S(2)}) copy-start(bf16[144,256]{1,0:T(8,128)(2,1)} %get-tuple-element.203) | copy-start | bytes 221188
  731.8 6.2 copy-start.13
  731.8 6.5 copy-start.21
  731.8 6.6 copy-start.22
  732.6 5.9 copy-start.12
  736.6 2.0 copy-start.15
  736.7 2.1 copy-start.20
  747.2 27.9 %all-to-all-start.1 = ((bf16[16,245,128]{2,1,0:T(8,128)(2,1)}), bf16[16,245,128]{2,1,0:T(8,128)(2,1)S(1)}, u32[]{:S(2)}, u32[]{:S(2)}) async-start(bf16[16,245,128]{2,1,0:T(8,128)(2,1)} %pair_sum.1), calls=%async_computation.1 | async-start | bytes 2031616 | tf_op jit(solution)/shard_map/all_to_all | solution.py:1390
  751.0 24.0 %copy-start.3 = (f32[8,31360]{1,0:T(8,128)S(1)}, f32[8,31360]{1,0:T(8,128)}, u32[]{:S(2)}) copy-start(f32[8,31360]{1,0:T(8,128)} %param.31) | copy-start | bytes 3010564
  751.0 24.0 %copy-start.5 = (f32[8,31360]{1,0:T(8,128)S(1)}, f32[8,31360]{1,0:T(8,128)}, u32[]{:S(2)}) copy-start(f32[8,31360]{1,0:T(8,128)} %param.32) | copy-start | bytes 3010564
  775.1 4.2 copy-start.4
  779.3 2.1 copy-start
  (7 other events, 9.5 us)
Sparse Core Ops, SparseCore 0:
  303.0 198.5 all-gather.1
